TPU v7x, 32 devices: a 4x4x1 block of a 4x4x8 slice. The times are simulated.
32 devices in a mesh: dp: 1 (over z), sp: 4 (over y), tp: 8 (over x, core).
Axes of the slice: x: 4, y: 4, z: 1, core: 2. Of those that a mesh axis runs over, the one named last changes fastest.
The devices are a block of a 4x4x8 slice.
Arguments:
- hidden_in: bfloat16 [4096, 3072], P(('dp', 'sp', 'tp'))
- segment_ids: int32 [4096], P(('dp', 'sp', 'tp'))
- positions: int32 [4096], P(('dp', 'sp', 'tp'))
- attn_gain: bfloat16 [4, 3072], replicated
- w_q: bfloat16 [4, 3072, 3072], P(None, None, 'tp')
- w_k: bfloat16 [4, 3072, 1024], P(None, None, 'tp')
- w_v: bfloat16 [4, 3072, 1024], P(None, None, 'tp')
- w_o: bfloat16 [4, 3072, 3072], P(None, 'tp')
- mlp_gain: bfloat16 [4, 3072], replicated
- w_gate: bfloat16 [4, 3072, 8192], P(None, None, 'tp')
- w_up: bfloat16 [4, 3072, 8192], P(None, None, 'tp')
- w_down: bfloat16 [4, 8192, 3072], P(None, 'tp')
Outputs:
- output 1: bfloat16 [4096, 3072], P(('dp', 'sp', 'tp'))
- output 2: bfloat16 [4, 4096, 8, 128], P(None, ('dp', 'sp'), 'tp')
- output 3: bfloat16 [4, 4096, 8, 128], P(None, ('dp', 'sp'), 'tp')
All inputs are finite; a program needn't handle non-finite values.
Results may differ from a plain program's by a relative error of at most 0.02.
Values are sent between devices in bfloat16 or wider.
A program may use at most 768 MiB of HBM per device.

v0:
```python
import math
import jax
import jax.numpy as jnp
from jax import lax
from jax.sharding import PartitionSpec as P

HEAD_DIM = 128
ROPE_BASE = 1e4
NORM_EPS = 1e-5
SCORE_SCALE = HEAD_DIM ** -0.5


def rms_norm(hidden, gain_vec):
    hidden32 = hidden.astype(jnp.float32)
    inv_rms = lax.rsqrt(jnp.mean(hidden32 * hidden32, axis=-1, keepdims=True) + NORM_EPS)
    return (hidden32 * inv_rms * gain_vec.astype(jnp.float32)).astype(jnp.bfloat16)


def rotary(rot_in, positions):
    half_dim = HEAD_DIM // 2
    inv_freq = ROPE_BASE ** (-jnp.arange(half_dim, dtype=jnp.float32) / half_dim)
    angles = positions.astype(jnp.float32)[..., None] * inv_freq
    cos_val = jnp.cos(angles)[..., None, :]
    sin_val = jnp.sin(angles)[..., None, :]
    first_half = rot_in[..., :half_dim]
    second_half = rot_in[..., half_dim:]
    return jnp.concatenate([first_half * cos_val - second_half * sin_val, second_half * cos_val + first_half * sin_val], axis=-1)


def attention_rows(q_rot, k_keys, v_keys, row_index, row_seg, key_seg):
    n_rows, n_kv, group_size = q_rot.shape[0], q_rot.shape[1], q_rot.shape[2]
    blk_rows = math.gcd(n_rows, 128)
    n_blocks = n_rows // blk_rows
    key_index = jnp.arange(k_keys.shape[0])

    def one_block(block_in):
        q_blk, idx_blk, seg_blk = block_in
        scores = jnp.einsum('qkgd,skd->kgqs', q_blk, k_keys, preferred_element_type=jnp.float32) * SCORE_SCALE
        allowed = (idx_blk[:, None] >= key_index[None, :]) & (seg_blk[:, None] == key_seg[None, :])
        probs = jax.nn.softmax(jnp.where(allowed, scores, -1e30), axis=-1).astype(jnp.bfloat16)
        return jnp.einsum('kgqs,skd->kgqd', probs, v_keys, preferred_element_type=jnp.float32).astype(jnp.bfloat16)

    blocks = (q_rot.reshape(n_blocks, blk_rows, n_kv, group_size, HEAD_DIM),
              row_index.reshape(n_blocks, blk_rows), row_seg.reshape(n_blocks, blk_rows))
    return lax.map(one_block, blocks)


def solution(mesh):
    n_tp = mesh.shape['tp']
    tok_spec = P(('dp', 'sp', 'tp'))
    col_spec = P(None, None, 'tp')
    row_spec = P(None, 'tp', None)
    cache_spec = P(None, ('dp', 'sp'), 'tp', None)

    def device_fn(hidden_in, segment_ids, positions, attn_gain, w_q, w_k, w_v, w_o, mlp_gain, w_gate, w_up, w_down):
        tok_local, model_dim = hidden_in.shape
        n_rows = tok_local * n_tp
        n_kv = w_k.shape[2] // HEAD_DIM
        group_size = w_q.shape[2] // HEAD_DIM // n_kv
        row_seg = lax.all_gather(segment_ids, 'tp', tiled=True)
        row_pos = lax.all_gather(positions, 'tp', tiled=True)
        key_seg = lax.all_gather(row_seg, 'sp', tiled=True)
        row_index = lax.axis_index('sp') * n_rows + jnp.arange(n_rows)
        hidden = hidden_in
        k_list = []
        v_list = []
        for layer_idx in range(w_q.shape[0]):
            normed = lax.all_gather(rms_norm(hidden, attn_gain[layer_idx]), 'tp', axis=0, tiled=True)
            q_lin = jnp.dot(normed, w_q[layer_idx], preferred_element_type=jnp.float32).reshape(n_rows, n_kv * group_size, HEAD_DIM)
            k_lin = jnp.dot(normed, w_k[layer_idx], preferred_element_type=jnp.float32).reshape(n_rows, n_kv, HEAD_DIM)
            v_rows = jnp.dot(normed, w_v[layer_idx], preferred_element_type=jnp.float32).astype(jnp.bfloat16).reshape(n_rows, n_kv, HEAD_DIM)
            q_rot = rotary(q_lin, row_pos).astype(jnp.bfloat16).reshape(n_rows, n_kv, group_size, HEAD_DIM)
            k_rows = rotary(k_lin, row_pos).astype(jnp.bfloat16)
            k_keys = lax.all_gather(k_rows, 'sp', axis=0, tiled=True)
            v_keys = lax.all_gather(v_rows, 'sp', axis=0, tiled=True)
            att_out = attention_rows(q_rot, k_keys, v_keys, row_index, row_seg, key_seg)
            wo_heads = w_o[layer_idx].reshape(n_kv, group_size, HEAD_DIM, model_dim)
            part_sum = jnp.einsum('nkgqd,kgdm->nqm', att_out, wo_heads, preferred_element_type=jnp.float32).astype(jnp.bfloat16).reshape(n_rows, model_dim)
            attn_res = lax.psum_scatter(part_sum, 'tp', scatter_dimension=0, tiled=True)
            hidden_mid = (hidden.astype(jnp.float32) + attn_res.astype(jnp.float32)).astype(jnp.bfloat16)
            normed_mlp = lax.all_gather(rms_norm(hidden_mid, mlp_gain[layer_idx]), 'tp', axis=0, tiled=True)
            gate_lin = jnp.dot(normed_mlp, w_gate[layer_idx], preferred_element_type=jnp.float32)
            up_lin = jnp.dot(normed_mlp, w_up[layer_idx], preferred_element_type=jnp.float32)
            act_vals = (jax.nn.silu(gate_lin) * up_lin).astype(jnp.bfloat16)
            down_part = jnp.dot(act_vals, w_down[layer_idx], preferred_element_type=jnp.float32).astype(jnp.bfloat16)
            mlp_res = lax.psum_scatter(down_part, 'tp', scatter_dimension=0, tiled=True)
            hidden = (hidden_mid.astype(jnp.float32) + mlp_res.astype(jnp.float32)).astype(jnp.bfloat16)
            k_list.append(k_rows)
            v_list.append(v_rows)
        return hidden, jnp.stack(k_list), jnp.stack(v_list)

    return jax.shard_map(device_fn, mesh=mesh,
                         in_specs=(P(('dp', 'sp', 'tp'), None), tok_spec, tok_spec, P(), col_spec, col_spec, col_spec, row_spec, P(), col_spec, col_spec, row_spec),
                         out_specs=(P(('dp', 'sp', 'tp'), None), cache_spec, cache_spec), check_vma=False)
```

profile of v0, /device:TPU:120, one launch (start us, length us, event | category | flops | bytes accessed | tf_op | source)
XLA Modules:
  0.0 1244.3 jit_solution(6778117972446703727)
XLA Ops:
  12.6 23.6 %all-gather.5 = s32[8,1,128]{2,1,0:T(1,128)S(1)} all-gather(s32[1,1,128]{2,1,0:T(1,128)} %bitcast.520), channel_id=1, replica_groups=mesh['dp'=1,'sp'=4,'tp'=8] {'tp'}, dimensions={0}, use_global_device_ids=true | all-gather | bytes 4608 | tf_op jit(solution)/shard_map/all_gather | solution.py:61
  125.0 35.6 %while.44 = (s32[]{:T(128)}, bf16[8,1,3,128,128]{4,3,2,1,0:T(8,128)(2,1)S(1)}, s32[8,128]{1,0:T(8,128)S(1)}, s32[8,128]{1,0:T(8,128)S(1)}, s32[4096]{0:T(1024)S(...) while((s32[]{:T(128)}, ...), condition=%wide.region_4.5_spmd.clone, body=%wide.region_1.4_spmd.clone.sunk | while | flops 819510528 | bytes 26439300 | solution.py:45
  169.0 39.0 %reduce-scatter.9.cloned.1.call-done = bf16[128,3072]{1,0:T(8,128)(2,1)} async-done(((bf16[1024,3072]{1,0:T(8,128)(2,1)}), bf16[128,3072]{1,0:T(8,128)(2,1)}) %reduce-scatter.9.cloned.1.call-update) | async-done | bytes 786448 | tf_op jit(solution)/shard_map/reduce_scatter | solution.py:79
  212.4 37.4 %all-gather.27.cloned.1.call-done = bf16[1024,3072]{1,0:T(8,128)(2,1)} async-done(((bf16[128,3072]{1,0:T(8,128)(2,1)}), bf16[1024,3072]{1,0:T(8,128)(2,1)}) %all-gather.27.cloned.1.call-update) | async-done | bytes 6291472 | tf_op jit(solution)/shard_map/all_gather | solution.py:81
  283.5 40.2 %reduce-scatter.11.cloned.1.call-done = bf16[128,3072]{1,0:T(8,128)(2,1)} async-done(((bf16[1024,3072]{1,0:T(8,128)(2,1)}), bf16[128,3072]{1,0:T(8,128)(2,1)}) %reduce-scatter.11.cloned.1.call-update) | async-done | bytes 786448 | tf_op jit(solution)/shard_map/reduce_scatter | solution.py:86
  326.6 37.8 %all-gather.29.cloned.1.call-done = bf16[1024,3072]{1,0:T(8,128)(2,1)} async-done(((bf16[128,3072]{1,0:T(8,128)(2,1)}), bf16[1024,3072]{1,0:T(8,128)(2,1)}) %all-gather.29.cloned.1.call-update) | async-done | bytes 6291472 | tf_op jit(solution)/shard_map/all_gather | solution.py:68
  393.8 21.8 %all-gather.49.cloned.1.call-done = bf16[4096,128]{1,0:T(8,128)(2,1)} async-done(((bf16[1024,128]{1,0:T(8,128)(2,1)}), bf16[4096,128]{1,0:T(8,128)(2,1)}) %all-gather.49.cloned.1.call-update) | async-done | bytes 1048592 | tf_op jit(solution)/shard_map/all_gather | solution.py:75
  416.7 45.7 %while.45 = (s32[]{:T(128)}, bf16[8,1,3,128,128]{4,3,2,1,0:T(8,128)(2,1)}, s32[8,128]{1,0:T(8,128)}, s32[8,128]{1,0:T(8,128)}, s32[4096]{0:T(1024)S(1)}, /*index...) while((s32[]{:T(128)}, ...), condition=%wide.region_12.13_spmd.clone, body=%wide.region_9.12_spmd.clone.sunk | while | flops 819510528 | bytes 26438784 | solution.py:45
  469.7 41.6 %reduce-scatter.13.cloned.1.call-done = bf16[128,3072]{1,0:T(8,128)(2,1)} async-done(((bf16[1024,3072]{1,0:T(8,128)(2,1)}), bf16[128,3072]{1,0:T(8,128)(2,1)}) %reduce-scatter.13.cloned.1.call-update) | async-done | bytes 786448 | tf_op jit(solution)/shard_map/reduce_scatter | solution.py:79
  515.4 37.6 %all-gather.33.cloned.1.call-done = bf16[1024,3072]{1,0:T(8,128)(2,1)} async-done(((bf16[128,3072]{1,0:T(8,128)(2,1)}), bf16[1024,3072]{1,0:T(8,128)(2,1)}) %all-gather.33.cloned.1.call-update) | async-done | bytes 6291472 | tf_op jit(solution)/shard_map/all_gather | solution.py:81
  586.7 40.2 %reduce-scatter.15.cloned.1.call-done = bf16[128,3072]{1,0:T(8,128)(2,1)} async-done(((bf16[1024,3072]{1,0:T(8,128)(2,1)}), bf16[128,3072]{1,0:T(8,128)(2,1)}) %reduce-scatter.15.cloned.1.call-update) | async-done | bytes 786448 | tf_op jit(solution)/shard_map/reduce_scatter | solution.py:86
  629.8 37.8 %all-gather.35.cloned.1.call-done = bf16[1024,3072]{1,0:T(8,128)(2,1)} async-done(((bf16[128,3072]{1,0:T(8,128)(2,1)}), bf16[1024,3072]{1,0:T(8,128)(2,1)}) %all-gather.35.cloned.1.call-update) | async-done | bytes 6291472 | tf_op jit(solution)/shard_map/all_gather | solution.py:68
  697.1 21.7 %all-gather.51.cloned.1.call-done = bf16[4096,128]{1,0:T(8,128)(2,1)} async-done(((bf16[1024,128]{1,0:T(8,128)(2,1)}), bf16[4096,128]{1,0:T(8,128)(2,1)}) %all-gather.51.cloned.1.call-update) | async-done | bytes 1048592 | tf_op jit(solution)/shard_map/all_gather | solution.py:75
  718.9 48.2 %while.46 = (s32[]{:T(128)}, bf16[8,1,3,128,128]{4,3,2,1,0:T(8,128)(2,1)S(1)}, s32[8,128]{1,0:T(8,128)}, s32[8,128]{1,0:T(8,128)}, s32[4096]{0:T(1024)S(1)}, /*i...) while((s32[]{:T(128)}, ...), condition=%wide.region_20.21_spmd.clone, body=%wide.region_17.20_spmd.clone.sunk | while | flops 819510528 | bytes 26439808 | solution.py:45
  774.1 41.6 %reduce-scatter.17.cloned.1.call-done = bf16[128,3072]{1,0:T(8,128)(2,1)} async-done(((bf16[1024,3072]{1,0:T(8,128)(2,1)}), bf16[128,3072]{1,0:T(8,128)(2,1)}) %reduce-scatter.17.cloned.1.call-update) | async-done | bytes 786448 | tf_op jit(solution)/shard_map/reduce_scatter | solution.py:79
  819.9 37.6 %all-gather.39.cloned.1.call-done = bf16[1024,3072]{1,0:T(8,128)(2,1)} async-done(((bf16[128,3072]{1,0:T(8,128)(2,1)}), bf16[1024,3072]{1,0:T(8,128)(2,1)}) %all-gather.39.cloned.1.call-update) | async-done | bytes 6291472 | tf_op jit(solution)/shard_map/all_gather | solution.py:81
  869.5 21.6 %fusion.138 = bf16[1024,3072]{1,0:T(8,128)(2,1)} fusion(bf16[4,1024,3072]{2,1,0:T(8,128)(2,1)} %param.31, f32[1024,1024]{1,0:T(8,128)} %fusion.98, bf16[1024,3072]{1,0:T(8,128)(2,1)} %all-gather.39.cloned.1.call-done, bf16[4,3072,1024]{2,1,0:T(8,128)(2,1)} %param.29), kind=kOutput, calls=%fused_computation.134 | convolution fusion | flops 12894339072 | bytes 29360128 | tf_op jit(solution)/shard_map/dot_general | solution.py:85
  891.2 40.2 %reduce-scatter.19.cloned.1.call-done = bf16[128,3072]{1,0:T(8,128)(2,1)} async-done(((bf16[1024,3072]{1,0:T(8,128)(2,1)}), bf16[128,3072]{1,0:T(8,128)(2,1)}) %reduce-scatter.19.cloned.1.call-update) | async-done | bytes 786448 | tf_op jit(solution)/shard_map/reduce_scatter | solution.py:86
  934.3 37.8 %all-gather.41.cloned.1.call-done = bf16[1024,3072]{1,0:T(8,128)(2,1)} async-done(((bf16[128,3072]{1,0:T(8,128)(2,1)}), bf16[1024,3072]{1,0:T(8,128)(2,1)}) %all-gather.41.cloned.1.call-update) | async-done | bytes 6291472 | tf_op jit(solution)/shard_map/all_gather | solution.py:68
  1001.5 21.8 %all-gather.53.cloned.1.call-done = bf16[4096,128]{1,0:T(8,128)(2,1)} async-done(((bf16[1024,128]{1,0:T(8,128)(2,1)}), bf16[4096,128]{1,0:T(8,128)(2,1)}) %all-gather.53.cloned.1.call-update) | async-done | bytes 1048592 | tf_op jit(solution)/shard_map/all_gather | solution.py:75
  1024.4 45.7 %while.47 = (s32[]{:T(128)}, bf16[8,1,3,128,128]{4,3,2,1,0:T(8,128)(2,1)}, s32[8,128]{1,0:T(8,128)}, s32[8,128]{1,0:T(8,128)}, s32[4096]{0:T(1024)S(1)}, /*index...) while((s32[]{:T(128)}, ...), condition=%wide.region_28.29_spmd.clone, body=%wide.region_25.28_spmd.clone.sunk | while | flops 819510528 | bytes 26438784 | solution.py:45
  1077.4 41.6 %reduce-scatter.21.cloned.1.call-done = bf16[128,3072]{1,0:T(8,128)(2,1)} async-done(((bf16[1024,3072]{1,0:T(8,128)(2,1)}), bf16[128,3072]{1,0:T(8,128)(2,1)}) %reduce-scatter.21.cloned.1.call-update) | async-done | bytes 786448 | tf_op jit(solution)/shard_map/reduce_scatter | solution.py:79
  1123.2 37.6 %all-gather.45.cloned.1.call-done = bf16[1024,3072]{1,0:T(8,128)(2,1)} async-done(((bf16[128,3072]{1,0:T(8,128)(2,1)}), bf16[1024,3072]{1,0:T(8,128)(2,1)}) %all-gather.45.cloned.1.call-update) | async-done | bytes 6291472 | tf_op jit(solution)/shard_map/all_gather | solution.py:81
  1200.1 34.6 %reduce-scatter.23.cloned.1.call-done = bf16[128,3072]{1,0:T(8,128)(2,1)} async-done(((bf16[1024,3072]{1,0:T(8,128)(2,1)}), bf16[128,3072]{1,0:T(8,128)(2,1)}) %reduce-scatter.23.cloned.1.call-update) | async-done | bytes 786448 | tf_op jit(solution)/shard_map/reduce_scatter | solution.py:86
  (479 shorter events, 534.8 us)
Async XLA Ops:
  7.2 44.9 %all-gather.23.cloned.1.call-start = ((), (), s32[]{:S(2)}) async-start(), calls=%async_computation.8 | async-start | bytes 7077888 | tf_op jit(solution)/shard_map/all_gather | solution.py:68
  12.5 110.7 %all-gather.25.cloned.1.call-start = ((), (), s32[]{:S(2)}) async-start(), calls=%async_computation.9 | async-start | bytes 1310720 | tf_op jit(solution)/shard_map/all_gather | solution.py:74
  59.9 65.0 %all-gather.47.cloned.1.call-start = ((), (), s32[]{:S(2)}) async-start(), calls=%async_computation.28 | async-start | bytes 1310720 | tf_op jit(solution)/shard_map/all_gather | solution.py:75
  78.6 129.4 %reduce-scatter.9.cloned.1.call-start = ((), (), s32[]{:S(2)}) async-start(), calls=%async_computation.10 | async-start | bytes 7077888 | tf_op jit(solution)/shard_map/reduce_scatter | solution.py:79
  167.7 82.1 %all-gather.27.cloned.1.call-start = ((), (), s32[]{:S(2)}) async-start(), calls=%async_computation.11 | async-start | bytes 7077888 | tf_op jit(solution)/shard_map/all_gather | solution.py:81
  211.9 111.8 %reduce-scatter.11.cloned.1.call-start = ((), (), s32[]{:S(2)}) async-start(), calls=%async_computation.12 | async-start | bytes 7077888 | tf_op jit(solution)/shard_map/reduce_scatter | solution.py:86
  283.4 81.0 %all-gather.29.cloned.1.call-start = ((), (), s32[]{:S(2)}) async-start(), calls=%async_computation.13 | async-start | bytes 7077888 | tf_op jit(solution)/shard_map/all_gather | solution.py:68
  326.6 65.6 %all-gather.31.cloned.1.call-start = ((), (), s32[]{:S(2)}) async-start(), calls=%async_computation.14 | async-start | bytes 1310720 | tf_op jit(solution)/shard_map/all_gather | solution.py:74
  371.6 44.0 %all-gather.49.cloned.1.call-start = ((), (), s32[]{:S(2)}) async-start(), calls=%async_computation.29 | async-start | bytes 1310720 | tf_op jit(solution)/shard_map/all_gather | solution.py:75
  377.4 133.9 %reduce-scatter.13.cloned.1.call-start = ((), (), s32[]{:S(2)}) async-start(), calls=%async_computation.15 | async-start | bytes 7077888 | tf_op jit(solution)/shard_map/reduce_scatter | solution.py:79
  469.6 83.4 %all-gather.33.cloned.1.call-start = ((), (), s32[]{:S(2)}) async-start(), calls=%async_computation.16 | async-start | bytes 7077888 | tf_op jit(solution)/shard_map/all_gather | solution.py:81
  515.1 111.8 %reduce-scatter.15.cloned.1.call-start = ((), (), s32[]{:S(2)}) async-start(), calls=%async_computation.17 | async-start | bytes 7077888 | tf_op jit(solution)/shard_map/reduce_scatter | solution.py:86
  586.6 81.0 %all-gather.35.cloned.1.call-start = ((), (), s32[]{:S(2)}) async-start(), calls=%async_computation.18 | async-start | bytes 7077888 | tf_op jit(solution)/shard_map/all_gather | solution.py:68
  629.8 65.7 %all-gather.37.cloned.1.call-start = ((), (), s32[]{:S(2)}) async-start(), calls=%async_computation.19 | async-start | bytes 1310720 | tf_op jit(solution)/shard_map/all_gather | solution.py:74
  674.9 43.9 %all-gather.51.cloned.1.call-start = ((), (), s32[]{:S(2)}) async-start(), calls=%async_computation.30 | async-start | bytes 1310720 | tf_op jit(solution)/shard_map/all_gather | solution.py:75
  680.4 135.3 %reduce-scatter.17.cloned.1.call-start = ((), (), s32[]{:S(2)}) async-start(), calls=%async_computation.20 | async-start | bytes 7077888 | tf_op jit(solution)/shard_map/reduce_scatter | solution.py:79
  774.1 83.4 %all-gather.39.cloned.1.call-start = ((), (), s32[]{:S(2)}) async-start(), calls=%async_computation.21 | async-start | bytes 7077888 | tf_op jit(solution)/shard_map/all_gather | solution.py:81
  819.6 111.8 %reduce-scatter.19.cloned.1.call-start = ((), (), s32[]{:S(2)}) async-start(), calls=%async_computation.22 | async-start | bytes 7077888 | tf_op jit(solution)/shard_map/reduce_scatter | solution.py:86
  891.2 81.0 %all-gather.41.cloned.1.call-start = ((), (), s32[]{:S(2)}) async-start(), calls=%async_computation.23 | async-start | bytes 7077888 | tf_op jit(solution)/shard_map/all_gather | solution.py:68
  934.3 65.7 %all-gather.43.cloned.1.call-start = ((), (), s32[]{:S(2)}) async-start(), calls=%async_computation.24 | async-start | bytes 1310720 | tf_op jit(solution)/shard_map/all_gather | solution.py:74
  979.4 44.0 %all-gather.53.cloned.1.call-start = ((), (), s32[]{:S(2)}) async-start(), calls=%async_computation.31 | async-start | bytes 1310720 | tf_op jit(solution)/shard_map/all_gather | solution.py:75
  985.1 133.9 %reduce-scatter.21.cloned.1.call-start = ((), (), s32[]{:S(2)}) async-start(), calls=%async_computation.25 | async-start | bytes 7077888 | tf_op jit(solution)/shard_map/reduce_scatter | solution.py:79
  1077.3 83.4 %all-gather.45.cloned.1.call-start = ((), (), s32[]{:S(2)}) async-start(), calls=%async_computation.26 | async-start | bytes 7077888 | tf_op jit(solution)/shard_map/all_gather | solution.py:81
  1122.8 111.8 %reduce-scatter.23.cloned.1.call-start = ((), (), s32[]{:S(2)}) async-start(), calls=%async_computation.27 | async-start | bytes 7077888 | tf_op jit(solution)/shard_map/reduce_scatter | solution.py:86
  (80 other events, 1010.7 us)
Sparse Core Ops, SparseCore 0:
  12.6 39.3 all-gather.22
  60.0 20.3 all-gather.24
  82.0 21.8 all-gather.46
  167.8 40.1 reduce-scatter.8
  212.0 37.7 all-gather.26
  283.6 40.1 reduce-scatter.10
  326.7 37.7 all-gather.28
  371.8 20.4 all-gather.30
  393.8 21.8 all-gather.48
  469.7 41.5 reduce-scatter.12
  515.3 37.7 all-gather.32
  586.8 40.0 reduce-scatter.14
  629.9 37.7 all-gather.34
  675.0 20.4 all-gather.36
  696.8 21.8 all-gather.50
  774.2 41.5 reduce-scatter.16
  819.7 37.7 all-gather.38
  891.3 40.0 reduce-scatter.18
  934.4 37.7 all-gather.40
  979.5 20.4 all-gather.42
  1001.5 21.8 all-gather.52
  1077.4 41.5 reduce-scatter.20
  1123.0 37.7 all-gather.44
  1194.5 40.1 reduce-scatter.22
where the time goes:
time: 1250 us; the launch traced here: 1240 us
  waiting for transfers between devices  676 us (54%)
  matrix products  330 us (26%)
  other arithmetic  94.5 us (8%)
  local copies, waits for them, and re-layouts  66.4 us (5%)
  blocking collectives  57 us (5%)
  between operations  15.7 us (1%)
    reduce_scatter x4, waiting for transfers between devices, device_fn(): attn_res = lax.psum_scatter(part_sum, 'tp', scatter_dimension=0, tiled=True)  164 us
    reduce_scatter x4, waiting for transfers between devices, device_fn(): mlp_res = lax.psum_scatter(down_part, 'tp', scatter_dimension=0, tiled=True)  155 us
    all_gather x4, waiting for transfers between devices, device_fn(): lax.all_gather(rms_norm(hidden_mid, mlp_gain[layer_idx]), 'tp', axis=0, t...  150 us
    all_gather x4, waiting for transfers between devices, device_fn(): lax.all_gather(rms_norm(hidden, attn_gain[layer_idx]), 'tp', axis=0, tile...  129 us
    dot_general x4, matrix products, device_fn(): jnp.dot(act_vals, w_down[layer_idx], preferred_element_type=jnp.float32)  86.4 us
    all_gather x4, waiting for transfers between devices, device_fn(): v_keys = lax.all_gather(v_rows, 'sp', axis=0, tiled=True)  65.3 us
    dot_general x32, matrix products, one_block(): jnp.einsum('qkgd,skd->kgqs', q_blk, k_keys, preferred_element_type=jnp.fl...  54.3 us
    dot_general x32, matrix products, one_block(): jnp.einsum('kgqs,skd->kgqd', probs, v_keys, preferred_element_type=jnp.fl...  48.8 us
  transfers between devices with their start and end apart: 24, of which 22 were waited for; matrix products, arithmetic and copies ran while one was open for 7% of the time, Pallas kernels for 0%

commit v1 on v0

v1 whole, which is shorter than its diff:
```python
import jax
import jax.numpy as jnp
from jax import lax
from jax.experimental import pallas as pl
from jax.experimental.pallas import tpu as pltpu
from jax.sharding import PartitionSpec as P

HEAD_DIM = 128
ROPE_BASE = 1e4
NORM_EPS = 1e-5
LOG2E = 1.4426950408889634
SCORE_EXP2 = HEAD_DIM ** -0.5 * LOG2E
NEG = -1e30
MESH = pl.DeviceIdType.MESH
F32 = jnp.float32
BF16 = jnp.bfloat16
CORES = 2
BATCHES = 2
OPP, RIGHT, LEFT, OWN = 0, 1, 2, 3


def dot(a, b):
    return jnp.dot(a, b, preferred_element_type=F32)


def make_kernel(n_layers, n_sp, n_tp, sub, model_dim, q_dim, ffn, col):
    chips = n_tp // CORES
    half = sub // 2
    unit = CORES * sub
    heads = q_dim // HEAD_DIM
    chip_rows = BATCHES * unit
    n_pair = chips // 2

    def kernel(hid, cos_t, sin_t, q_seg, k_seg, own_seg, gain_a, gain_m, wq_h, wk_h, wv_h, wo_h, wg_h, wu_h, wd_h,
               out, k_out, v_out,
               res, gath, part, acc_rs, opp_in, nb_in, act, q_buf, m_buf, l_buf, o_buf, kv,
               w_qkv, w_o, w_g, w_u, w_d,
               w_sem, ag_send, ag_sib, ag_l, ag_r, ag_o, ag_sf, rs_dsend, rs_sib, rs_send, rs_opp, rs_nb, kv_send, kv_recv, c_sem):
        y = lax.axis_index('sp')
        me = lax.axis_index('tp')
        x = me // CORES
        c = lax.rem(me, CORES)
        oc = 1 - c
        xl = lax.rem(x + chips - 1, chips)
        xr = lax.rem(x + 1, chips)
        xo = lax.rem(x + 2, chips)
        unit_of = {OPP: xo, RIGHT: xr, LEFT: xl, OWN: x}
        sib = {'tp': x * CORES + oc}
        right = {'tp': xr * CORES + c}
        left = {'tp': xl * CORES + c}
        lo = pl.ds(0, half)
        hi = pl.ds(half, half)

        def rdma(src, dst, ssem, rsem, dev):
            return pltpu.make_async_remote_copy(src_ref=src, dst_ref=dst, send_sem=ssem, recv_sem=rsem,
                                                device_id=dev, device_id_type=MESH)

        def attn_weights(l):
            return [pltpu.make_async_copy(wq_h.at[l], w_qkv.at[:, pl.ds(0, q_dim)], w_sem.at[0]),
                    pltpu.make_async_copy(wk_h.at[l], w_qkv.at[:, pl.ds(q_dim, HEAD_DIM)], w_sem.at[1]),
                    pltpu.make_async_copy(wv_h.at[l], w_qkv.at[:, pl.ds(q_dim + HEAD_DIM, HEAD_DIM)], w_sem.at[2]),
                    pltpu.make_async_copy(wo_h.at[l], w_o, w_sem.at[3])]

        def mlp_weights(l):
            return [pltpu.make_async_copy(wg_h.at[l], w_g, w_sem.at[4]),
                    pltpu.make_async_copy(wu_h.at[l], w_u, w_sem.at[5]),
                    pltpu.make_async_copy(wd_h.at[l], w_d, w_sem.at[6])]

        for cp in attn_weights(0) + mlp_weights(0):
            cp.start()

        barrier = pltpu.get_barrier_semaphore()
        for dev in (sib, right, left):
            pl.semaphore_signal(barrier, inc=1, device_id=dev, device_id_type=MESH)
        for d in range(1, n_sp):
            pl.semaphore_signal(barrier, inc=1, device_id={'sp': lax.rem(y + d, n_sp)}, device_id_type=MESH)
        pl.semaphore_wait(barrier, 3 + n_sp - 1)

        def ag_copies(b):
            own = gath.at[b, x, c]
            return {
                'sib': rdma(own, own, ag_send.at[b, 0], ag_sib.at[b], sib),
                'r_lo': rdma(own.at[lo], own.at[lo], ag_send.at[b, 1], ag_l.at[b, 0], right),
                'l_hi': rdma(own.at[hi], own.at[hi], ag_send.at[b, 2], ag_r.at[b, 1], left),
                'r_hi': rdma(own.at[hi], own.at[hi], ag_send.at[b, 3], ag_l.at[b, 1], right),
                'l_lo': rdma(own.at[lo], own.at[lo], ag_send.at[b, 4], ag_r.at[b, 0], left),
                'f_r': rdma(gath.at[b, xl, c, lo], gath.at[b, xl, c, lo], ag_send.at[b, 5], ag_o.at[b, 0], right),
                'f_l': rdma(gath.at[b, xr, c, hi], gath.at[b, xr, c, hi], ag_send.at[b, 6], ag_o.at[b, 1], left),
                's_l': rdma(gath.at[b, xl, c], gath.at[b, xl, c], ag_send.at[b, 7], ag_sf.at[b, LEFT], sib),
                's_r': rdma(gath.at[b, xr, c], gath.at[b, xr, c], ag_send.at[b, 8], ag_sf.at[b, RIGHT], sib),
                's_o': rdma(gath.at[b, xo, c], gath.at[b, xo, c], ag_send.at[b, 9], ag_sf.at[b, OPP], sib),
            }

        def arrived(ref, sem):
            rdma(ref, ref, ag_send.at[0, 0], sem, sib).wait_recv()

        def ag0a(b):
            cps = ag_copies(b)
            for name in ('sib', 'r_lo', 'l_hi'):
                cps[name].start()

        def ag0b(b):
            cps = ag_copies(b)
            for name in ('r_hi', 'l_lo'):
                cps[name].start()

        def ag1(b):
            cps = ag_copies(b)
            arrived(gath.at[b, xl, c, lo], ag_l.at[b, 0])
            cps['f_r'].start()
            arrived(gath.at[b, xr, c, hi], ag_r.at[b, 1])
            cps['f_l'].start()

        def ag2(b):
            cps = ag_copies(b)
            arrived(gath.at[b, xl, c, hi], ag_l.at[b, 1])
            cps['s_l'].start()
            arrived(gath.at[b, xr, c, lo], ag_r.at[b, 0])
            cps['s_r'].start()

        def ag3(b):
            cps = ag_copies(b)
            arrived(gath.at[b, xo, c, lo], ag_o.at[b, 0])
            arrived(gath.at[b, xo, c, hi], ag_o.at[b, 1])
            cps['s_o'].start()

        def ag_unit_ready(b, k):
            arrived(gath.at[b, unit_of[k], oc], ag_sib.at[b] if k == OWN else ag_sf.at[b, k])

        def ag_sent(b):
            for cp in ag_copies(b).values():
                cp.wait_send()

        def rs_pair(b, k):
            return rdma(part.at[k, oc], acc_rs.at[b, k], rs_dsend.at[b, k], rs_sib.at[b, k], sib)

        def rs_copies(b):
            return {
                'o_r': rdma(acc_rs.at[b, OPP, lo], opp_in.at[b, 0], rs_send.at[b, 0], rs_opp.at[b, 0], right),
                'o_l': rdma(acc_rs.at[b, OPP, hi], opp_in.at[b, 1], rs_send.at[b, 1], rs_opp.at[b, 1], left),
                'r_hi': rdma(acc_rs.at[b, RIGHT, hi], nb_in.at[b, 0, hi], rs_send.at[b, 2], rs_nb.at[b, 0, 1], right),
                'l_lo': rdma(acc_rs.at[b, LEFT, lo], nb_in.at[b, 1, lo], rs_send.at[b, 3], rs_nb.at[b, 1, 0], left),
                'r_lo': rdma(acc_rs.at[b, RIGHT, lo], nb_in.at[b, 0, lo], rs_send.at[b, 4], rs_nb.at[b, 0, 0], right),
                'l_hi': rdma(acc_rs.at[b, LEFT, hi], nb_in.at[b, 1, hi], rs_send.at[b, 5], rs_nb.at[b, 1, 1], left),
            }

        def pair_sum(b, k):
            cp = rs_pair(b, k)
            cp.wait_send()
            cp.wait_recv()
            acc_rs[b, k] = (acc_rs[b, k].astype(F32) + part[k, c].astype(F32)).astype(BF16)

        def rs1(b):
            pair_sum(b, OPP)
            cps = rs_copies(b)
            cps['o_r'].start()
            cps['o_l'].start()

        def rs2a(b):
            cps = rs_copies(b)
            pair_sum(b, RIGHT)
            cps['r_hi'].start()
            pair_sum(b, LEFT)
            cps['l_lo'].start()
            pair_sum(b, OWN)

        def rs2b(b):
            cps = rs_copies(b)
            cps['o_r'].wait_recv()
            acc_rs[b, RIGHT, lo] = (acc_rs[b, RIGHT, lo].astype(F32) + opp_in[b, 0].astype(F32)).astype(BF16)
            cps['r_lo'].start()
            cps['o_l'].wait_recv()
            acc_rs[b, LEFT, hi] = (acc_rs[b, LEFT, hi].astype(F32) + opp_in[b, 1].astype(F32)).astype(BF16)
            cps['l_hi'].start()

        def fin(b):
            cps = rs_copies(b)
            for name in ('r_hi', 'l_lo', 'r_lo', 'l_hi'):
                cps[name].wait_recv()
            for cp in cps.values():
                cp.wait_send()
            total = (acc_rs[b, OWN].astype(F32) + nb_in[b, 0].astype(F32) + nb_in[b, 1].astype(F32)).astype(BF16)
            res[b] = (res[b].astype(F32) + total.astype(F32)).astype(BF16)

        def norm(b, gain):
            h = res[b].astype(F32)
            inv = lax.rsqrt(jnp.mean(h * h, axis=-1, keepdims=True) + NORM_EPS)
            gath[b, x, c] = (h * inv * gain).astype(BF16)

        def store_part(k, lhs, w, n):
            cols = pl.ds(pl.multiple_of(n * col, col), col)
            r = dot(lhs, w[:, cols]).astype(BF16)
            part[k, :, :, cols] = r.reshape(CORES, sub, col)

        def rope(v, b, u):
            return v * cos_t[u, b] + pltpu.roll(v, HEAD_DIM // 2, 1) * sin_t[u, b]

        def qkv(l, b, k):
            ag_unit_ready(b, k)
            u = unit_of[k]
            n = gath[b, u].reshape(unit, model_dim)
            for h0 in range(0, heads + 2, 2):
                width = min(2, heads + 2 - h0) * HEAD_DIM
                r = dot(n, w_qkv[:, pl.ds(h0 * HEAD_DIM, width)])
                for h in range(h0, min(h0 + 2, heads + 2)):
                    v = r[:, (h - h0) * HEAD_DIM:(h - h0 + 1) * HEAD_DIM]
                    if h < heads:
                        q_buf[b, k, h] = rope(v, b, u).astype(BF16)
                    elif h == heads:
                        kv[l, y, u, b, :, :, pl.ds(0, HEAD_DIM)] = rope(v, b, u).astype(BF16).reshape(CORES, sub, HEAD_DIM)
                    else:
                        kv[l, y, u, b, :, :, pl.ds(HEAD_DIM, HEAD_DIM)] = v.astype(BF16).reshape(CORES, sub, HEAD_DIM)
            m_buf[b, k] = jnp.full(m_buf.shape[2:], NEG, F32)
            l_buf[b, k] = jnp.zeros(l_buf.shape[2:], F32)
            o_buf[b, k] = jnp.zeros(o_buf.shape[2:], F32)
            for d in range(1, n_sp):
                @pl.when(y + d < n_sp)
                def _():
                    kv_copy(l, kv.at[l, y, u, b], d).start()

        def kv_copy(l, ref, d):
            return rdma(ref, ref, kv_send.at[d - 1], kv_recv.at[l, y], {'sp': lax.min(y + d, n_sp - 1)})

        def cache_copies(l):
            cps = []
            for b in range(BATCHES):
                for core in range(CORES):
                    for i, ref in enumerate((k_out, v_out)):
                        cps.append(pltpu.make_async_copy(kv.at[l, y, :, b, core, :, pl.ds(i * HEAD_DIM, HEAD_DIM)],
                                                         ref.at[l, :, core, b], c_sem.at[b, core, i]))
            return cps

        def flash(b, k, keys, vals, mask):
            n_keys = keys.shape[0]
            q = q_buf[b, k].reshape(heads * unit, HEAD_DIM)
            s = lax.dot_general(q, keys, (((1,), (1,)), ((), ())), preferred_element_type=F32)
            s = jnp.where(mask[None], s.reshape(heads, unit, n_keys), NEG).reshape(heads * unit, n_keys)
            m_old = m_buf[b, k]
            m_new = jnp.maximum(m_old, jnp.max(s, axis=-1, keepdims=True))
            alpha = jnp.exp2((m_old - m_new) * SCORE_EXP2)
            p = jnp.exp2((s - jnp.concatenate([m_new] * (n_keys // HEAD_DIM), axis=1)) * SCORE_EXP2)
            m_buf[b, k] = m_new
            total = l_buf[b, k] * alpha
            for i in range(n_keys // HEAD_DIM):
                total = total + p[:, i * HEAD_DIM:(i + 1) * HEAD_DIM]
            l_buf[b, k] = total
            o_buf[b, k] = o_buf[b, k] * alpha + dot(p.astype(BF16), vals)

        def attn_rows_below(l, b, k, on):
            u = unit_of[k]

            def step(j, carry):
                block = kv[l, j // n_pair, pl.ds(lax.rem(j, n_pair) * 2, 2)].reshape(2 * chip_rows, 2 * HEAD_DIM)
                seg = jnp.concatenate([q_seg[u, b]] * (2 * chip_rows // HEAD_DIM), axis=1)
                mask = seg == jnp.broadcast_to(k_seg[j], (unit, 2 * chip_rows))
                flash(b, k, block[:, :HEAD_DIM], block[:, HEAD_DIM:], mask)
                return carry

            lax.fori_loop(0, jnp.where(on, y * n_pair, 0), step, 0)

        def kv_ready(l, on):
            for r in range(n_sp - 1):
                @pl.when(jnp.logical_and(on, r < y))
                def _():
                    rdma(kv.at[l, r], kv.at[l, r], kv_send.at[0], kv_recv.at[l, r], sib).wait_recv()

        def attn_own(l, b, k):
            u = unit_of[k]
            row = lax.broadcasted_iota(jnp.int32, (unit, chip_rows), 0)
            lane = lax.broadcasted_iota(jnp.int32, (unit, chip_rows), 1)
            q_tok = u * chip_rows + row // sub * (BATCHES * sub) + b * sub + lax.rem(row, sub)
            k_tok = lax.rem(lane, unit) // sub * (BATCHES * sub) + lane // unit * sub + lax.rem(lane, sub)

            def step(j, carry):
                block = kv[l, y, j].reshape(chip_rows, 2 * HEAD_DIM)
                seg = jnp.concatenate([q_seg[u, b]] * (chip_rows // HEAD_DIM), axis=1)
                mask = jnp.logical_and(seg == jnp.broadcast_to(own_seg[j], (unit, chip_rows)), q_tok >= k_tok + j * chip_rows)
                flash(b, k, block[:, :HEAD_DIM], block[:, HEAD_DIM:], mask)
                return carry

            lax.fori_loop(0, u + 1, step, 0)

        def attn_out(b, k):
            inv = 1.0 / jnp.sum(l_buf[b, k], axis=-1, keepdims=True)
            o = (o_buf[b, k] * inv).astype(BF16)
            o = jnp.concatenate([o[h * unit:(h + 1) * unit] for h in range(heads)], axis=1)

            def step(n, carry):
                store_part(k, o, w_o, n)
                return carry

            lax.fori_loop(0, model_dim // col, step, 0)
            rs_pair(b, k).start()

        ffn_col = min(256, ffn)

        def gate_up(b, k):
            ag_unit_ready(b, k)
            n = gath[b, unit_of[k]].reshape(unit, model_dim)

            def step(j, carry):
                cols = pl.ds(pl.multiple_of(j * ffn_col, ffn_col), ffn_col)
                g = dot(n, w_g[:, cols])
                act[b, k, :, cols] = (g * jax.nn.sigmoid(g) * dot(n, w_u[:, cols])).astype(BF16)
                return carry

            lax.fori_loop(0, ffn // ffn_col, step, 0)

        def down(b, k):
            def step(n, carry):
                store_part(k, act[b, k], w_d, n)
                return carry

            lax.fori_loop(0, model_dim // col, step, 0)
            rs_pair(b, k).start()

        A, B = 0, 1
        res[...] = hid[...]
        norm(A, gain_a[0])
        ag0a(A)
        ag0b(A)

        def layer(l, carry):
            more = l + 1 < n_layers
            nxt = lax.min(l + 1, n_layers - 1)
            later = l > 0
            for cp in attn_weights(l)[:3]:
                cp.wait()
            qkv(l, A, OWN)

            @pl.when(later)
            def _():
                fin(B)
            norm(B, gain_a[l])
            ag0a(B)
            ag1(A)
            ag0b(B)
            ag2(A)
            qkv(l, A, LEFT)
            qkv(l, A, RIGHT)
            kv_ready(l, later)
            attn_rows_below(l, A, OWN, later)
            ag3(A)
            qkv(l, B, OWN)
            ag1(B)
            qkv(l, A, OPP)
            attn_rows_below(l, A, LEFT, later)
            attn_rows_below(l, A, RIGHT, later)
            ag2(B)
            qkv(l, B, LEFT)
            qkv(l, B, RIGHT)
            attn_rows_below(l, A, OPP, later)
            attn_rows_below(l, B, OWN, later)
            ag3(B)
            attn_rows_below(l, B, LEFT, later)
            qkv(l, B, OPP)
            for cp in cache_copies(l):
                cp.start()
            kv_ready(l, jnp.logical_not(later))
            for k in (OPP, RIGHT, LEFT, OWN):
                attn_rows_below(l, A, k, jnp.logical_not(later))
            attn_weights(l)[3].wait()
            ag_sent(A)
            attn_own(l, A, OPP)
            attn_out(A, OPP)
            attn_own(l, A, RIGHT)
            attn_out(A, RIGHT)
            rs1(A)
            attn_own(l, A, LEFT)
            attn_out(A, LEFT)
            attn_own(l, A, OWN)
            attn_out(A, OWN)
            rs2a(A)
            ag_sent(B)
            attn_rows_below(l, B, OPP, True)
            attn_own(l, B, OPP)
            attn_out(B, OPP)
            rs2b(A)
            attn_rows_below(l, B, RIGHT, True)
            attn_own(l, B, RIGHT)
            attn_out(B, RIGHT)
            rs1(B)
            attn_rows_below(l, B, LEFT, jnp.logical_not(later))
            attn_own(l, B, LEFT)
            attn_out(B, LEFT)
            attn_rows_below(l, B, OWN, jnp.logical_not(later))
            attn_own(l, B, OWN)
            attn_out(B, OWN)

            @pl.when(more)
            def _():
                for cp in attn_weights(nxt):
                    cp.start()
            rs2a(B)
            fin(A)
            norm(A, gain_m[l])
            ag0a(A)
            rs2b(B)
            ag0b(A)

            for cp in mlp_weights(l)[:2]:
                cp.wait()
            gate_up(A, OWN)
            fin(B)
            norm(B, gain_m[l])
            ag0a(B)
            ag1(A)
            ag0b(B)
            ag2(A)
            gate_up(A, LEFT)
            gate_up(A, RIGHT)
            ag3(A)
            gate_up(B, OWN)
            ag1(B)
            gate_up(A, OPP)
            mlp_weights(l)[2].wait()
            ag_sent(A)
            down(A, OPP)
            down(A, RIGHT)
            rs1(A)
            down(A, LEFT)
            down(A, OWN)
            ag2(B)
            rs2a(A)
            gate_up(B, LEFT)
            gate_up(B, RIGHT)
            ag3(B)
            gate_up(B, OPP)
            ag_sent(B)
            down(B, OPP)
            down(B, RIGHT)
            rs2b(A)
            rs1(B)
            down(B, LEFT)
            down(B, OWN)

            @pl.when(more)
            def _():
                for cp in mlp_weights(nxt):
                    cp.start()
            rs2a(B)
            fin(A)

            @pl.when(more)
            def _():
                norm(A, gain_a[nxt])
                ag0a(A)
            rs2b(B)

            @pl.when(more)
            def _():
                ag0b(A)
            for cp in cache_copies(l):
                cp.wait()
            for d in range(1, n_sp):
                @pl.when(y + d < n_sp)
                def _():
                    kv_copy(l, kv.at[l, y], d).wait_send()
            return carry

        lax.fori_loop(0, n_layers, layer, 0)
        fin(B)
        out[...] = res[...]

    return kernel


def solution(mesh):
    n_sp, n_tp = mesh.shape['sp'], mesh.shape['tp']
    chips = n_tp // CORES
    tok_spec = P(('dp', 'sp', 'tp'))
    col_spec = P(None, None, 'tp')
    row_spec = P(None, 'tp', None)
    cache_spec = P(None, ('dp', 'sp'), 'tp', None)

    def device_fn(hidden_in, segment_ids, positions, attn_gain, w_q, w_k, w_v, w_o, mlp_gain, w_gate, w_up, w_down):
        tok_local, model_dim = hidden_in.shape
        n_layers, _, q_dim = w_q.shape
        ffn = w_gate.shape[2]
        sub = tok_local // BATCHES
        unit = CORES * sub
        n_rows = tok_local * n_tp
        heads = q_dim // HEAD_DIM
        col = min(512, model_dim)

        marks = lax.all_gather(jnp.stack([segment_ids, positions]), ('sp', 'tp'))
        marks = marks.reshape(n_sp, chips, CORES, 2, BATCHES, sub).transpose(3, 0, 1, 4, 2, 5)
        segs = marks[0]
        row = lax.axis_index('sp')
        own_seg = lax.dynamic_index_in_dim(segs, row, 0, False)
        own_pos = lax.dynamic_index_in_dim(marks[1], row, 0, False)
        half_dim = HEAD_DIM // 2
        inv_freq = ROPE_BASE ** (-jnp.arange(half_dim, dtype=F32) / half_dim)
        angles = own_pos.reshape(chips, BATCHES, unit, 1).astype(F32) * inv_freq
        cos_v, sin_v = jnp.cos(angles), jnp.sin(angles)
        cos_t = jnp.concatenate([cos_v, cos_v], axis=-1)
        sin_t = jnp.concatenate([-sin_v, sin_v], axis=-1)
        q_seg = jnp.broadcast_to(own_seg.reshape(chips, BATCHES, unit, 1), (chips, BATCHES, unit, HEAD_DIM))
        k_seg = segs.reshape(n_sp * chips // 2, 1, 2 * BATCHES * unit)
        o_seg = own_seg.reshape(chips, 1, BATCHES * unit)

        vmem = pl.BlockSpec(memory_space=pltpu.VMEM)
        hbm = pl.BlockSpec(memory_space=pl.ANY)
        dma = pltpu.SemaphoreType.DMA
        rows_q = heads * unit
        cache = jax.ShapeDtypeStruct((n_layers, chips, CORES, BATCHES, sub, HEAD_DIM), BF16)
        out, k_c, v_c = pl.pallas_call(
            make_kernel(n_layers, n_sp, n_tp, sub, model_dim, q_dim, ffn, col),
            name='decoder_stack',
            out_shape=(jax.ShapeDtypeStruct((BATCHES, sub, model_dim), BF16), cache, cache),
            in_specs=[vmem] * 8 + [hbm] * 7,
            out_specs=(vmem, hbm, hbm),
            scratch_shapes=[
                pltpu.VMEM((BATCHES, sub, model_dim), BF16),
                pltpu.VMEM((BATCHES, chips, CORES, sub, model_dim), BF16),
                pltpu.VMEM((4, CORES, sub, model_dim), BF16),
                pltpu.VMEM((BATCHES, 4, sub, model_dim), BF16),
                pltpu.VMEM((BATCHES, 2, sub // 2, model_dim), BF16),
                pltpu.VMEM((BATCHES, 2, sub, model_dim), BF16),
                pltpu.VMEM((BATCHES, 4, unit, ffn), BF16),
                pltpu.VMEM((BATCHES, 4, heads, unit, HEAD_DIM), BF16),
                pltpu.VMEM((BATCHES, 4, rows_q, HEAD_DIM), F32),
                pltpu.VMEM((BATCHES, 4, rows_q, HEAD_DIM), F32),
                pltpu.VMEM((BATCHES, 4, rows_q, HEAD_DIM), F32),
                pltpu.VMEM((n_layers, n_sp, chips, BATCHES, CORES, sub, 2 * HEAD_DIM), BF16),
                pltpu.VMEM((model_dim, q_dim + 2 * HEAD_DIM), BF16),
                pltpu.VMEM((q_dim, model_dim), BF16),
                pltpu.VMEM((model_dim, ffn), BF16),
                pltpu.VMEM((model_dim, ffn), BF16),
                pltpu.VMEM((ffn, model_dim), BF16),
                dma((7,)),
                dma((BATCHES, 10)), dma((BATCHES,)), dma((BATCHES, 2)), dma((BATCHES, 2)), dma((BATCHES, 2)), dma((BATCHES, 3)),
                dma((BATCHES, 4)), dma((BATCHES, 4)), dma((BATCHES, 6)), dma((BATCHES, 2)), dma((BATCHES, 2, 2)),
                dma((n_sp - 1,)), dma((n_layers, n_sp)), dma((BATCHES, CORES, 2)),
            ],
            compiler_params=pltpu.CompilerParams(collective_id=0, has_side_effects=True, vmem_limit_bytes=67_000_000),
        )(hidden_in.reshape(BATCHES, sub, model_dim), cos_t, sin_t, q_seg, k_seg, o_seg,
          attn_gain.astype(F32).reshape(n_layers, 1, model_dim), mlp_gain.astype(F32).reshape(n_layers, 1, model_dim),
          w_q, w_k, w_v, w_o, w_gate, w_up, w_down)
        cache_shape = (n_layers, n_rows, 1, HEAD_DIM)
        return out.reshape(tok_local, model_dim), k_c.reshape(cache_shape), v_c.reshape(cache_shape)

    return jax.shard_map(device_fn, mesh=mesh,
                         in_specs=(P(('dp', 'sp', 'tp'), None), tok_spec, tok_spec, P(), col_spec, col_spec, col_spec, row_spec, P(), col_spec, col_spec, row_spec),
                         out_specs=(P(('dp', 'sp', 'tp'), None), cache_spec, cache_spec), check_vma=False)
```

time: 1250 us -> 681 us (0.54)
  waiting for transfers between devices: 676 us -> 0 us
  Pallas kernels: 0 us -> 631 us
  matrix products: 330 us -> 0 us
  other arithmetic: 94.5 us -> 4.6 us
  local copies, waits for them, and re-layouts: 66.4 us -> 12 us
  blocking collectives: 57 us -> 32.8 us
  between operations: 15.7 us -> 0.69 us
    pallas_call x0 -> x1, Pallas kernels: none -> 631 us  [device_fn(): pl.pallas_call(make_kernel(n_layers, n_sp, n_tp, sub, model_dim, q_dim, f...]
    all_gather x16 -> x0, waiting for transfers between devices: 356 us -> none  [the longest x4 150 us: device_fn(): lax.all_gather(rms_norm(hidden_mid, mlp_gain[layer_idx]), 'tp', axis=0, t...]
    dot_general x88 -> x0, matrix products: 330 us -> none  [the longest x4 86.4 us: device_fn(): jnp.dot(act_vals, w_down[layer_idx], preferred_element_type=jnp.float32)]
    reduce_scatter x8 -> x0, waiting for transfers between devices: 319 us -> none  [the longest x4 164 us: device_fn(): attn_res = lax.psum_scatter(part_sum, 'tp', scatter_dimension=0, tiled=True)]
    reduce_sum x40 -> x0, other arithmetic: 43.6 us -> none  [the longest x32 31.6 us: one_block(): jax.nn.softmax(jnp.where(allowed, scores, -1e+30), axis=-1)]
    all_gather x3 -> x1, blocking collectives: 57 us -> 32.8 us  [device_fn(): marks = lax.all_gather(jnp.stack([segment_ids, positions]), ('sp', 'tp'))]
    dot_general x5 -> x0, local copies, waits for them, and re-layouts: 18.6 us -> none  [device_fn(): jnp.dot(normed, w_q[layer_idx], preferred_element_type=jnp.float32)]
    convert_element_type x10 -> x1, other arithmetic: 17.4 us -> 0.01 us  [device_fn(): angles = own_pos.reshape(chips, BATCHES, unit, 1).astype(F32) * inv_freq]
  transfers between devices with their start and end apart: 24 -> 0, of which waited for: 22 -> 0; matrix products, arithmetic and copies ran while one was open for 7% -> 0% of each run, Pallas kernels for 0% -> 0%
where the time goes in v1:
time: 681 us
  Pallas kernels  631 us (93%)
  blocking collectives  32.8 us (5%)
  local copies, waits for them, and re-layouts  12 us (2%)
    pallas_call x1, Pallas kernels, device_fn(): pl.pallas_call(make_kernel(n_layers, n_sp, n_tp, sub, model_dim, q_dim, f...  631 us
    all_gather x1, blocking collectives, device_fn(): marks = lax.all_gather(jnp.stack([segment_ids, positions]), ('sp', 'tp'))  32.8 us

profile of v1, /device:TPU:120, one launch (start us, length us, event | category | flops | bytes accessed | tf_op | source)
XLA Modules:
  0.0 680.7 jit_solution(10661776518834018955)
XLA Ops:
  0.6 0.7 add_bitcast_fusion
  1.3 32.8 %all-gather.1 = s32[32,2,128]{2,1,0:T(2,128)S(1)} all-gather(s32[1,2,128]{2,1,0:T(2,128)S(1)} %add_bitcast_fusion), channel_id=2, replica_groups=mesh['dp'=1,'sp'=4,'tp'=8] {'sp','tp'}, dimensions={0}, use_global_device_ids=true | all-gather | bytes 33792 | tf_op jit(solution)/shard_map/all_gather | solution.py:486
  34.2 0.1 reshape.59
  34.4 0.7 reshape_squeeze.3.k_seg
  35.1 0.1 convert_element_type.14
  35.1 0.7 reshape.60.own_seg
  35.8 0.1 broadcast_in_dim.8
  35.9 1.4 reshape.69.gain_a
  37.3 1.4 reshape.71.gain_m
  38.7 1.0 broadcast_in_dim.9.q_seg
  39.7 1.9 fusion
  41.6 1.0 pad_maximum_fusion.1.sin_t
  42.6 1.0 pad_maximum_fusion.cos_t
  43.6 630.6 %decoder_stack.1 = (bf16[2,64,3072]{2,1,0:T(8,128)(2,1)}, bf16[4,4,2,2,64,128]{5,4,3,2,1,0:T(8,128)(2,1)}, bf16[4,4,2,2,64,128]{5,4,3,2,1,0:T(8,128)(2,1)}) custom-call(bf16[2,64,3072]{2,1,0:T(8,128)(2,1)} %bitcast.17, f32[4,2,128,128]{3,2,1,0:T(8,128)} %pad_maximum_fusion.cos_t, f32[4,2,128,128]{3,2,1,0:T(8,128)} %pad_maximum_fusion.1.sin_t, ...), custom_call_target="tpu_custom_call" | custom-call | tf_op jit(solution)/shard_map/decoder_stack/pallas_call | solution.py:507
  674.1 2.1 copy.26
  676.2 2.3 copy.27
  678.5 2.3 copy.28
  (4 shorter events, 0.1 us)

commit v2 on v1

v2 whole, which is shorter than its diff:
```python
import jax
import jax.numpy as jnp
from jax import lax
from jax.experimental import pallas as pl
from jax.experimental.pallas import tpu as pltpu
from jax.sharding import PartitionSpec as P

HEAD_DIM = 128
ROPE_BASE = 1e4
NORM_EPS = 1e-5
LOG2E = 1.4426950408889634
SCORE_EXP2 = HEAD_DIM ** -0.5 * LOG2E
NEG = -1e30
SPLIT = 2.0 ** 99
MESH = pl.DeviceIdType.MESH
F32 = jnp.float32
BF16 = jnp.bfloat16
CORES = 2
BATCHES = 2
OPP, RIGHT, LEFT, OWN = 0, 1, 2, 3


def dot(a, b):
    return jnp.dot(a, b, preferred_element_type=F32)


def make_kernel(n_layers, n_sp, n_tp, sub, model_dim, q_dim, ffn, col):
    chips = n_tp // CORES
    half = sub // 2
    unit = CORES * sub
    heads = q_dim // HEAD_DIM
    chip_rows = BATCHES * unit

    def kernel(hid, tab_own, hot_own, gain_a, gain_m, wq_h, wk_h, wv_h, wo_h, wg_h, wu_h, wd_h,
               out, k_out, v_out,
               res, gath, part, acc_rs, opp_in, nb_in, act, q_buf, m_buf, l_buf, o_buf, kv, tab, hot,
               w_qkv, w_o, w_g, w_u, w_d,
               w_sem, ag_send, ag_sib, ag_l, ag_r, ag_o, ag_sf, rs_dsend, rs_sib, rs_send, rs_opp, rs_nb, kv_send, kv_recv, c_sem, t_send, t_recv, h_send, h_recv, e_send, e_recv):
        y = lax.axis_index('sp')
        me = lax.axis_index('tp')
        x = me // CORES
        c = lax.rem(me, CORES)
        oc = 1 - c
        xl = lax.rem(x + chips - 1, chips)
        xr = lax.rem(x + 1, chips)
        xo = lax.rem(x + 2, chips)

        def unit_of(k):
            if isinstance(k, int):
                return (xo, xr, xl, x)[k]
            p, i = k // 2, lax.rem(k, 2)
            return lax.rem(x + (2 + p) * (1 - i) + (1 - p) * i, chips)
        sib = {'tp': x * CORES + oc}
        right = {'tp': xr * CORES + c}
        left = {'tp': xl * CORES + c}
        lo = pl.ds(0, half)
        hi = pl.ds(half, half)

        def rdma(src, dst, ssem, rsem, dev):
            return pltpu.make_async_remote_copy(src_ref=src, dst_ref=dst, send_sem=ssem, recv_sem=rsem,
                                                device_id=dev, device_id_type=MESH)

        def attn_weights(l):
            return [pltpu.make_async_copy(wq_h.at[l], w_qkv.at[:, pl.ds(0, q_dim)], w_sem.at[0]),
                    pltpu.make_async_copy(wk_h.at[l], w_qkv.at[:, pl.ds(q_dim, HEAD_DIM)], w_sem.at[1]),
                    pltpu.make_async_copy(wv_h.at[l], w_qkv.at[:, pl.ds(q_dim + HEAD_DIM, HEAD_DIM)], w_sem.at[2]),
                    pltpu.make_async_copy(wo_h.at[l], w_o, w_sem.at[3])]

        def mlp_weights(l):
            return [pltpu.make_async_copy(wg_h.at[l], w_g, w_sem.at[4]),
                    pltpu.make_async_copy(wu_h.at[l], w_u, w_sem.at[5]),
                    pltpu.make_async_copy(wd_h.at[l], w_d, w_sem.at[6])]

        for cp in attn_weights(0) + mlp_weights(0):
            cp.start()

        barrier = pltpu.get_barrier_semaphore()
        for t in range(1, n_tp):
            pl.semaphore_signal(barrier, inc=1, device_id={'tp': lax.rem(me + t, n_tp)}, device_id_type=MESH)
        for d in range(1, n_sp):
            pl.semaphore_signal(barrier, inc=1, device_id={'sp': lax.rem(y + d, n_sp)}, device_id_type=MESH)
        pl.semaphore_wait(barrier, n_tp - 1 + n_sp - 1)

        def ag_copies(b):
            own = gath.at[b, x, c]
            return {
                'sib': lambda: rdma(own, own, ag_send.at[b, 0], ag_sib.at[b], sib),
                'r_lo': lambda: rdma(own.at[lo], own.at[lo], ag_send.at[b, 1], ag_l.at[b, 0], right),
                'l_hi': lambda: rdma(own.at[hi], own.at[hi], ag_send.at[b, 2], ag_r.at[b, 1], left),
                'r_hi': lambda: rdma(own.at[hi], own.at[hi], ag_send.at[b, 3], ag_l.at[b, 1], right),
                'l_lo': lambda: rdma(own.at[lo], own.at[lo], ag_send.at[b, 4], ag_r.at[b, 0], left),
                'f_r': lambda: rdma(gath.at[b, xl, c, lo], gath.at[b, xl, c, lo], ag_send.at[b, 5], ag_o.at[b, 0], right),
                'f_l': lambda: rdma(gath.at[b, xr, c, hi], gath.at[b, xr, c, hi], ag_send.at[b, 6], ag_o.at[b, 1], left),
                's_l': lambda: rdma(gath.at[b, xl, c], gath.at[b, xl, c], ag_send.at[b, 7], ag_sf.at[b, LEFT], sib),
                's_r': lambda: rdma(gath.at[b, xr, c], gath.at[b, xr, c], ag_send.at[b, 8], ag_sf.at[b, RIGHT], sib),
                's_o': lambda: rdma(gath.at[b, xo, c], gath.at[b, xo, c], ag_send.at[b, 9], ag_sf.at[b, OPP], sib),
            }

        def arrived(ref, sem):
            rdma(ref, ref, ag_send.at[0, 0], sem, sib).wait_recv()

        def ag0a(b):
            cps = ag_copies(b)
            for name in ('sib', 'r_lo', 'l_hi'):
                cps[name]().start()

        def ag0b(b):
            cps = ag_copies(b)
            for name in ('r_hi', 'l_lo'):
                cps[name]().start()

        def ag1(b):
            cps = ag_copies(b)
            arrived(gath.at[b, xl, c, lo], ag_l.at[b, 0])
            cps['f_r']().start()
            arrived(gath.at[b, xr, c, hi], ag_r.at[b, 1])
            cps['f_l']().start()

        def ag2(b):
            cps = ag_copies(b)
            arrived(gath.at[b, xl, c, hi], ag_l.at[b, 1])
            cps['s_l']().start()
            arrived(gath.at[b, xr, c, lo], ag_r.at[b, 0])
            cps['s_r']().start()

        def ag3(b):
            cps = ag_copies(b)
            arrived(gath.at[b, xo, c, lo], ag_o.at[b, 0])
            arrived(gath.at[b, xo, c, hi], ag_o.at[b, 1])
            cps['s_o']().start()

        def ag_unit_ready(b, k):
            arrived(gath.at[b, unit_of(k), oc], ag_sib.at[b] if isinstance(k, int) and k == OWN else ag_sf.at[b, k])

        def ag_sent(b):
            for cp in ag_copies(b).values():
                cp().wait_send()

        def rs_pair(b, k):
            return rdma(part.at[k, oc], acc_rs.at[b, k], rs_dsend.at[b, k], rs_sib.at[b, k], sib)

        def rs_copies(b):
            return {
                'o_r': lambda: rdma(acc_rs.at[b, OPP, lo], opp_in.at[b, 0], rs_send.at[b, 0], rs_opp.at[b, 0], right),
                'o_l': lambda: rdma(acc_rs.at[b, OPP, hi], opp_in.at[b, 1], rs_send.at[b, 1], rs_opp.at[b, 1], left),
                'r_hi': lambda: rdma(acc_rs.at[b, RIGHT, hi], nb_in.at[b, 0, hi], rs_send.at[b, 2], rs_nb.at[b, 0, 1], right),
                'l_lo': lambda: rdma(acc_rs.at[b, LEFT, lo], nb_in.at[b, 1, lo], rs_send.at[b, 3], rs_nb.at[b, 1, 0], left),
                'r_lo': lambda: rdma(acc_rs.at[b, RIGHT, lo], nb_in.at[b, 0, lo], rs_send.at[b, 4], rs_nb.at[b, 0, 0], right),
                'l_hi': lambda: rdma(acc_rs.at[b, LEFT, hi], nb_in.at[b, 1, hi], rs_send.at[b, 5], rs_nb.at[b, 1, 1], left),
            }

        def pair_sum(b, k):
            cp = rs_pair(b, k)
            cp.wait_send()
            cp.wait_recv()
            acc_rs[b, k] = (acc_rs[b, k].astype(F32) + part[k, c].astype(F32)).astype(BF16)

        def rs1(b):
            pair_sum(b, OPP)
            cps = rs_copies(b)
            cps['o_r']().start()
            cps['o_l']().start()

        def rs2a(b):
            cps = rs_copies(b)
            pair_sum(b, RIGHT)
            cps['r_hi']().start()
            pair_sum(b, LEFT)
            cps['l_lo']().start()
            pair_sum(b, OWN)

        def rs2b(b):
            cps = rs_copies(b)
            cps['o_r']().wait_recv()
            acc_rs[b, RIGHT, lo] = (acc_rs[b, RIGHT, lo].astype(F32) + opp_in[b, 0].astype(F32)).astype(BF16)
            cps['r_lo']().start()
            cps['o_l']().wait_recv()
            acc_rs[b, LEFT, hi] = (acc_rs[b, LEFT, hi].astype(F32) + opp_in[b, 1].astype(F32)).astype(BF16)
            cps['l_hi']().start()

        def fin(b):
            cps = rs_copies(b)
            for name in ('r_hi', 'l_lo', 'r_lo', 'l_hi'):
                cps[name]().wait_recv()
            for cp in cps.values():
                cp().wait_send()
            total = (acc_rs[b, OWN].astype(F32) + nb_in[b, 0].astype(F32) + nb_in[b, 1].astype(F32)).astype(BF16)
            res[b] = (res[b].astype(F32) + total.astype(F32)).astype(BF16)

        def norm(b, gain):
            h = res[b].astype(F32)
            inv = lax.rsqrt(jnp.mean(h * h, axis=-1, keepdims=True) + NORM_EPS)
            gath[b, x, c] = (h * inv * gain).astype(BF16)

        def gain_row(ref, l):
            row = ref[0:1]
            for i in range(1, n_layers):
                row = jnp.where(l == i, ref[i:i + 1], row)
            return row

        def store_part(k, lhs, w, n):
            cols = pl.ds(n * col if isinstance(n, int) else pl.multiple_of(n * col, col), col)
            r = dot(lhs, w[:, cols]).astype(BF16)
            part[k, :, :, cols] = r.reshape(CORES, sub, col)

        def rope(v, cos_v, sin_v):
            return v * cos_v + pltpu.roll(v, HEAD_DIM // 2, 1) * sin_v

        def qkv(l, b, k):
            ag_unit_ready(b, k)
            u = unit_of(k)
            n = gath[b, u].reshape(unit, model_dim)
            packed = tab[b, u].reshape(unit, HEAD_DIM)
            swapped = pltpu.roll(packed, HEAD_DIM // 2, 1)
            first = lax.broadcasted_iota(jnp.int32, (unit, HEAD_DIM), 1) < HEAD_DIM // 2
            cos_v = jnp.where(first, packed, swapped)
            sin_v = jnp.where(first, -swapped, packed)
            away = ((hot[y, b, u].reshape(unit, HEAD_DIM).astype(F32) - 1.0) * SPLIT).astype(BF16)
            for h0 in range(0, heads + 2, 2):
                width = min(2, heads + 2 - h0) * HEAD_DIM
                r = dot(n, w_qkv[:, pl.ds(h0 * HEAD_DIM, width)])
                for h in range(h0, min(h0 + 2, heads + 2)):
                    v = r[:, (h - h0) * HEAD_DIM:(h - h0 + 1) * HEAD_DIM]
                    if h < heads:
                        q_buf[b, k, h, :, pl.ds(0, HEAD_DIM)] = rope(v, cos_v, sin_v).astype(BF16)
                        q_buf[b, k, h, :, pl.ds(HEAD_DIM, HEAD_DIM)] = away
                    elif h == heads:
                        kv[l, y, b, u, :, :, pl.ds(0, HEAD_DIM)] = rope(v, cos_v, sin_v).astype(BF16).reshape(CORES, sub, HEAD_DIM)
                    else:
                        kv[l, y, b, u, :, :, pl.ds(HEAD_DIM, HEAD_DIM)] = v.astype(BF16).reshape(CORES, sub, HEAD_DIM)
            m_buf[b, k] = jnp.full(m_buf.shape[2:], NEG, F32)
            l_buf[b, k] = jnp.zeros(l_buf.shape[2:], F32)
            o_buf[b, k] = jnp.zeros(o_buf.shape[2:], F32)
            for d in range(1, n_sp):
                @pl.when(y + d < n_sp)
                def _():
                    kv_copy(b, l, kv.at[l, y, b, u], d).start()

        def kv_copy(b, l, ref, d):
            return rdma(ref, ref, kv_send.at[b, d - 1], kv_recv.at[l, y, b], {'sp': lax.min(y + d, n_sp - 1)})

        def cache_copies(l):
            cps = []
            for b in range(BATCHES):
                for core in range(CORES):
                    for i, ref in enumerate((k_out, v_out)):
                        cps.append(pltpu.make_async_copy(kv.at[l, y, b, :, core, :, pl.ds(i * HEAD_DIM, HEAD_DIM)],
                                                         ref.at[l, :, core, b], c_sem.at[b, core, i]))
            return cps

        def flash(b, ks, block, marks, masks=None):
            n_keys = block.shape[0]
            keys = jnp.concatenate([block[:, :HEAD_DIM], marks], axis=1)
            vals = block[:, HEAD_DIM:]
            scores = [lax.dot_general(keys, q_buf[b, k].reshape(heads * unit, 2 * HEAD_DIM), (((1,), (1,)), ((), ())),
                                      preferred_element_type=F32) for k in ks]
            for i, k in enumerate(ks):
                s = scores[i]
                if masks is not None:
                    s = jnp.where(masks[i], s, NEG)
                m_old = m_buf[b, k]
                m_new = jnp.maximum(m_old, jnp.max(s, axis=0, keepdims=True))
                alpha = jnp.exp2((m_old - m_new) * SCORE_EXP2)
                p = jnp.exp2((s - m_new[0:1]) * SCORE_EXP2)
                m_buf[b, k] = m_new
                l_buf[b, k] = l_buf[b, k] * alpha + jnp.sum(p.reshape(n_keys // 8, 8, heads * unit), axis=0)
                o_buf[b, k] = o_buf[b, k] * alpha[0:1] + lax.dot_general(vals, p.astype(BF16), (((0,), (0,)), ((), ())),
                                                                         preferred_element_type=F32)

        def row_block(l, r, kb):
            return kv[l, r, kb].reshape(chips * unit, 2 * HEAD_DIM), hot[r, kb].reshape(chips * unit, HEAD_DIM)

        def attn_below(l, b, p, kb):
            def step(r, carry):
                flash(b, (2 * p, 2 * p + 1), *row_block(l, r, kb))
                return carry

            lax.fori_loop(0, y, step, 0)

        def kv_ready(l, kb):
            for r in range(n_sp - 1):
                @pl.when(r < y)
                def _():
                    rdma(kv.at[l, r, kb], kv.at[l, r, kb], kv_send.at[0, 0], kv_recv.at[l, r, kb], sib).wait_recv()

        def attn_own(l, b, p, kb):
            key = lax.broadcasted_iota(jnp.int32, (chips * unit, unit), 0)
            qry = lax.broadcasted_iota(jnp.int32, (chips * unit, unit), 1)
            ahead = (qry // sub - key // sub) * (BATCHES * sub) + lax.rem(qry, sub) - lax.rem(key, sub) + (b - kb) * sub
            ks = (2 * p, 2 * p + 1)
            masks = [jnp.concatenate([ahead >= -unit_of(k) * chip_rows] * heads, axis=1) for k in ks]
            flash(b, ks, *row_block(l, y, kb), masks)

        def attn_out(b, p):
            def one(i, carry):
                k = 2 * p + i
                o = o_buf[b, k] * (1.0 / jnp.sum(l_buf[b, k], axis=0, keepdims=True))
                o = jnp.concatenate([o[:, h * unit:(h + 1) * unit].T.astype(BF16) for h in range(heads)], axis=1)
                for n in range(model_dim // col):
                    store_part(k, o, w_o, n)
                rs_pair(b, k).start()
                return carry

            lax.fori_loop(0, 2, one, 0)

        ffn_col = min(1024, ffn)

        def gate_up(b, k):
            ag_unit_ready(b, k)
            n = gath[b, unit_of(k)].reshape(unit, model_dim)

            def step(j, carry):
                cols = pl.ds(j * ffn_col, ffn_col)
                g = dot(n, w_g[:, cols])
                act[b, k, :, cols] = (g * jax.nn.sigmoid(g) * dot(n, w_u[:, cols])).astype(BF16)
                return carry

            for j in range(ffn // ffn_col):
                step(j, 0)

        def down(b, p):
            def one(i, carry):
                k = 2 * p + i
                for n in range(model_dim // col):
                    store_part(k, act[b, k], w_d, n)
                rs_pair(b, k).start()
                return carry

            lax.fori_loop(0, 2, one, 0)

        def sides(fn, b):
            def one(i, carry):
                fn(b, LEFT - i)
                return carry

            lax.fori_loop(0, 2, one, 0)

        A, B = 0, 1
        res[...] = hid[...]
        norm(A, gain_row(gain_a, 0))
        ag0a(A)
        tab[:, x, c] = tab_own[...]
        hot[y, :, x, c] = hot_own[...]

        def peer_copies(t, src):
            to = {'tp': lax.rem(me + t, n_tp)}
            return (rdma(tab_own, tab.at[:, src // CORES, lax.rem(src, CORES)], t_send.at[t], t_recv.at[src], to),
                    rdma(hot_own, hot.at[y, :, src // CORES, lax.rem(src, CORES)], h_send.at[t], h_recv.at[src], to))

        def hot_copy(d):
            return rdma(hot.at[y], hot.at[y], e_send.at[d - 1], e_recv.at[y], {'sp': lax.min(y + d, n_sp - 1)})

        for t in range(1, n_tp):
            for cp in peer_copies(t, me):
                cp.start()
        for t in range(1, n_tp):
            for cp in peer_copies(t, lax.rem(me + t, n_tp)):
                cp.wait_recv()
        for d in range(1, n_sp):
            @pl.when(y + d < n_sp)
            def _():
                hot_copy(d).start()

        def layer(l, carry):
            more = l + 1 < n_layers
            nxt = lax.min(l + 1, n_layers - 1)
            for cp in attn_weights(l)[:3]:
                cp.wait()
            def qkv_l(b, k):
                qkv(l, b, k)

            qkv(l, A, OWN)

            @pl.when(l > 0)
            def _():
                rs2b(B)
            ag0b(A)
            ag1(A)

            @pl.when(l > 0)
            def _():
                fin(B)
            norm(B, gain_row(gain_a, l))
            ag0a(B)
            ag2(A)
            ag0b(B)
            sides(qkv_l, A)
            ag3(A)
            qkv(l, B, OWN)
            ag1(B)
            qkv(l, A, OPP)

            @pl.when(l == 0)
            def _():
                for r in range(n_sp - 1):
                    @pl.when(r < y)
                    def _():
                        rdma(hot.at[r], hot.at[r], e_send.at[0], e_recv.at[r], sib).wait_recv()
            kv_ready(l, A)

            def early(p, carry):
                attn_below(l, A, p, A)
                attn_own(l, A, p, A)
                return carry

            lax.fori_loop(0, 2, early, 0)
            ag2(B)
            sides(qkv_l, B)
            ag3(B)
            attn_weights(l)[3].wait()
            ag_sent(A)
            qkv(l, B, OPP)
            for cp in cache_copies(l):
                cp.start()

            def late_a(p, carry):
                attn_own(l, A, p, B)

                @pl.when(p == 0)
                def _():
                    kv_ready(l, B)
                attn_below(l, A, p, B)
                attn_out(A, p)

                @pl.when(p == 0)
                def _():
                    rs1(A)
                return carry

            lax.fori_loop(0, 2, late_a, 0)
            rs2a(A)
            ag_sent(B)

            def late_b(p, carry):
                def keys(kb, carry):
                    attn_below(l, B, p, kb)
                    attn_own(l, B, p, kb)
                    return carry

                lax.fori_loop(0, BATCHES, keys, 0)

                @pl.when(p == 0)
                def _():
                    rs2b(A)
                attn_out(B, p)

                @pl.when(p == 0)
                def _():
                    rs1(B)
                return carry

            lax.fori_loop(0, 2, late_b, 0)

            @pl.when(more)
            def _():
                for cp in attn_weights(nxt):
                    cp.start()
            fin(A)
            norm(A, gain_row(gain_m, l))
            rs2a(B)
            ag0a(A)
            for cp in mlp_weights(l)[:2]:
                cp.wait()
            gate_up(A, OWN)
            rs2b(B)
            ag0b(A)
            ag1(A)
            fin(B)
            norm(B, gain_row(gain_m, l))
            ag0a(B)
            ag2(A)
            ag0b(B)
            sides(gate_up, A)
            ag3(A)
            gate_up(B, OWN)
            ag1(B)
            gate_up(A, OPP)
            mlp_weights(l)[2].wait()
            ag_sent(A)
            down(A, 0)
            rs1(A)
            down(A, 1)
            ag2(B)
            gate_up(B, RIGHT)
            rs2a(A)
            ag3(B)
            gate_up(B, OPP)
            ag_sent(B)
            down(B, 0)
            rs2b(A)
            rs1(B)
            gate_up(B, LEFT)
            down(B, 1)

            @pl.when(more)
            def _():
                for cp in mlp_weights(nxt):
                    cp.start()
            rs2a(B)
            fin(A)

            @pl.when(more)
            def _():
                norm(A, gain_row(gain_a, nxt))
                ag0a(A)
            for cp in cache_copies(l):
                cp.wait()
            for d in range(1, n_sp):
                @pl.when(y + d < n_sp)
                def _():
                    for b in range(BATCHES):
                        kv_copy(b, l, kv.at[l, y, b], d).wait_send()
            return carry

        lax.fori_loop(0, n_layers, layer, 0)
        rs2b(B)
        fin(B)
        out[...] = res[...]
        for t in range(1, n_tp):
            for cp in peer_copies(t, me):
                cp.wait_send()
        for d in range(1, n_sp):
            @pl.when(y + d < n_sp)
            def _():
                hot_copy(d).wait_send()

    return kernel


def solution(mesh):
    n_sp, n_tp = mesh.shape['sp'], mesh.shape['tp']
    chips = n_tp // CORES
    tok_spec = P(('dp', 'sp', 'tp'))
    col_spec = P(None, None, 'tp')
    row_spec = P(None, 'tp', None)
    cache_spec = P(None, ('dp', 'sp'), 'tp', None)

    def device_fn(hidden_in, segment_ids, positions, attn_gain, w_q, w_k, w_v, w_o, mlp_gain, w_gate, w_up, w_down):
        tok_local, model_dim = hidden_in.shape
        n_layers, _, q_dim = w_q.shape
        ffn = w_gate.shape[2]
        sub = tok_local // BATCHES
        unit = CORES * sub
        n_rows = tok_local * n_tp
        heads = q_dim // HEAD_DIM
        col = min(1536, model_dim)

        half_dim = HEAD_DIM // 2
        inv_freq = ROPE_BASE ** (-jnp.arange(half_dim, dtype=F32) / half_dim)
        angles = positions.reshape(BATCHES, sub, 1).astype(F32) * inv_freq
        tab = jnp.concatenate([jnp.cos(angles), jnp.sin(angles)], axis=-1)
        hot = (segment_ids.reshape(BATCHES, sub, 1) == jnp.arange(HEAD_DIM)).astype(BF16)

        vmem = pl.BlockSpec(memory_space=pltpu.VMEM)
        hbm = pl.BlockSpec(memory_space=pl.ANY)
        dma = pltpu.SemaphoreType.DMA
        rows_q = heads * unit
        cache = jax.ShapeDtypeStruct((n_layers, chips, CORES, BATCHES, sub, HEAD_DIM), BF16)
        out, k_c, v_c = pl.pallas_call(
            make_kernel(n_layers, n_sp, n_tp, sub, model_dim, q_dim, ffn, col),
            name='decoder_stack',
            out_shape=(jax.ShapeDtypeStruct((BATCHES, sub, model_dim), BF16), cache, cache),
            in_specs=[vmem] * 5 + [hbm] * 7,
            out_specs=(vmem, hbm, hbm),
            scratch_shapes=[
                pltpu.VMEM((BATCHES, sub, model_dim), BF16),
                pltpu.VMEM((BATCHES, chips, CORES, sub, model_dim), BF16),
                pltpu.VMEM((4, CORES, sub, model_dim), BF16),
                pltpu.VMEM((BATCHES, 4, sub, model_dim), BF16),
                pltpu.VMEM((BATCHES, 2, sub // 2, model_dim), BF16),
                pltpu.VMEM((BATCHES, 2, sub, model_dim), BF16),
                pltpu.VMEM((BATCHES, 4, unit, ffn), BF16),
                pltpu.VMEM((BATCHES, 4, heads, unit, 2 * HEAD_DIM), BF16),
                pltpu.VMEM((BATCHES, 4, 8, rows_q), F32),
                pltpu.VMEM((BATCHES, 4, 8, rows_q), F32),
                pltpu.VMEM((BATCHES, 4, HEAD_DIM, rows_q), F32),
                pltpu.VMEM((n_layers, n_sp, BATCHES, chips, CORES, sub, 2 * HEAD_DIM), BF16),
                pltpu.VMEM((BATCHES, chips, CORES, sub, HEAD_DIM), F32),
                pltpu.VMEM((n_sp, BATCHES, chips, CORES, sub, HEAD_DIM), BF16),
                pltpu.VMEM((model_dim, q_dim + 2 * HEAD_DIM), BF16),
                pltpu.VMEM((q_dim, model_dim), BF16),
                pltpu.VMEM((model_dim, ffn), BF16),
                pltpu.VMEM((model_dim, ffn), BF16),
                pltpu.VMEM((ffn, model_dim), BF16),
                dma((7,)),
                dma((BATCHES, 10)), dma((BATCHES,)), dma((BATCHES, 2)), dma((BATCHES, 2)), dma((BATCHES, 2)), dma((BATCHES, 3)),
                dma((BATCHES, 4)), dma((BATCHES, 4)), dma((BATCHES, 6)), dma((BATCHES, 2)), dma((BATCHES, 2, 2)),
                dma((BATCHES, n_sp - 1)), dma((n_layers, n_sp, BATCHES)), dma((BATCHES, CORES, 2)),
                dma((n_tp,)), dma((n_tp,)), dma((n_tp,)), dma((n_tp,)), dma((n_sp - 1,)), dma((n_sp,)),
            ],
            compiler_params=pltpu.CompilerParams(collective_id=0, has_side_effects=True, vmem_limit_bytes=67_000_000),
        )(hidden_in.reshape(BATCHES, sub, model_dim), tab, hot, attn_gain.astype(F32), mlp_gain.astype(F32),
          w_q, w_k, w_v, w_o, w_gate, w_up, w_down)
        cache_shape = (n_layers, n_rows, 1, HEAD_DIM)
        return out.reshape(tok_local, model_dim), k_c.reshape(cache_shape), v_c.reshape(cache_shape)

    return jax.shard_map(device_fn, mesh=mesh,
                         in_specs=(P(('dp', 'sp', 'tp'), None), tok_spec, tok_spec, P(), col_spec, col_spec, col_spec, row_spec, P(), col_spec, col_spec, row_spec),
                         out_specs=(P(('dp', 'sp', 'tp'), None), cache_spec, cache_spec), check_vma=False)
```

time: 681 us -> 548 us (0.80)
  Pallas kernels: 631 us -> 535 us
  blocking collectives: 32.8 us -> 0 us
    pallas_call x1, Pallas kernels: 631 us -> 535 us  [device_fn(): pl.pallas_call(make_kernel(n_layers, n_sp, n_tp, sub, model_dim, q_dim, f...]
    all_gather x1 -> x0, blocking collectives: 32.8 us -> none  [device_fn(): marks = lax.all_gather(jnp.stack([segment_ids, positions]), ('sp', 'tp'))]
where the time goes in v2:
time: 548 us
  Pallas kernels  535 us (98%)
  local copies, waits for them, and re-layouts  7.41 us (1%)
    pallas_call x1, Pallas kernels, device_fn(): pl.pallas_call(make_kernel(n_layers, n_sp, n_tp, sub, model_dim, q_dim, f...  535 us

profile of v2, /device:TPU:120, one launch (start us, length us, event | category | flops | bytes accessed | tf_op | source)
XLA Modules:
  0.0 548.0 jit_solution(17070845136135327037)
XLA Ops:
  0.6 0.7 convert_element_type.20
  1.3 0.1 convert_element_type.21
  1.4 0.7 eq.15
  2.1 0.7 fusion.hot_own
  2.8 1.4 convert_element_type.23.gain_a
  4.2 1.4 convert_element_type.24.gain_m
  5.5 0.3 multiply_cosine_fusion
  5.9 0.7 pad_maximum_fusion.tab_own
  6.6 534.8 %decoder_stack.1 = (bf16[2,64,3072]{2,1,0:T(8,128)(2,1)}, bf16[4,4,2,2,64,128]{5,4,3,2,1,0:T(8,128)(2,1)}, bf16[4,4,2,2,64,128]{5,4,3,2,1,0:T(8,128)(2,1)}) custom-call(bf16[2,64,3072]{2,1,0:T(8,128)(2,1)} %bitcast.10, f32[2,64,128]{2,1,0:T(8,128)} %pad_maximum_fusion.tab_own, bf16[2,64,128]{2,1,0:T(8,128)(2,1)} %fusion.hot_own, ...), custom_call_target="tpu_custom_call" | custom-call | tf_op jit(solution)/shard_map/decoder_stack/pallas_call | solution.py:559
  541.4 2.1 copy.20
  543.4 2.3 copy.21
  545.7 2.3 copy.22
  (1 shorter events, 0.0 us)

commit v3 on v2

--- a/solution.py
+++ b/solution.py
@@ -193,9 +193,10 @@
             gath[b, x, c] = (h * inv * gain).astype(BF16)
 
         def gain_row(ref, l):
-            row = ref[0:1]
+            rows = ref[...].astype(F32)
+            row = rows[0:1]
             for i in range(1, n_layers):
-                row = jnp.where(l == i, ref[i:i + 1], row)
+                row = jnp.where(l == i, rows[i:i + 1], row)
             return row
 
         def store_part(k, lhs, w, n):
@@ -270,26 +271,42 @@
         def row_block(l, r, kb):
             return kv[l, r, kb].reshape(chips * unit, 2 * HEAD_DIM), hot[r, kb].reshape(chips * unit, HEAD_DIM)
 
-        def attn_below(l, b, p, kb):
+        def whole_row(l, r):
+            n = BATCHES * chips * unit
+            return kv[l, r].reshape(n, 2 * HEAD_DIM), hot[r].reshape(n, HEAD_DIM)
+
+        def attn_below(l, b, ks, a0, a1, b0, b1):
+            n_a = a1 - a0
+
+            def step(n, carry):
+                kb = jnp.where(n >= n_a, 1, 0)
+                flash(b, ks, *row_block(l, n + a0 + kb * (b0 - n_a - a0), kb))
+                return carry
+
+            lax.fori_loop(0, n_a + b1 - b0, step, 0)
+
+        def attn_below_rows(l, b, ks):
             def step(r, carry):
-                flash(b, (2 * p, 2 * p + 1), *row_block(l, r, kb))
+                flash(b, ks, *whole_row(l, r))
                 return carry
 
             lax.fori_loop(0, y, step, 0)
 
-        def kv_ready(l, kb):
+        def kv_ready(l, kb, first, last):
             for r in range(n_sp - 1):
-                @pl.when(r < y)
+                @pl.when(jnp.logical_and(r >= first, r < last))
                 def _():
                     rdma(kv.at[l, r, kb], kv.at[l, r, kb], kv_send.at[0, 0], kv_recv.at[l, r, kb], sib).wait_recv()
 
-        def attn_own(l, b, p, kb):
-            key = lax.broadcasted_iota(jnp.int32, (chips * unit, unit), 0)
-            qry = lax.broadcasted_iota(jnp.int32, (chips * unit, unit), 1)
-            ahead = (qry // sub - key // sub) * (BATCHES * sub) + lax.rem(qry, sub) - lax.rem(key, sub) + (b - kb) * sub
-            ks = (2 * p, 2 * p + 1)
+        def attn_own(l, b, ks, kb=None):
+            n_keys = chips * unit * (BATCHES if kb is None else 1)
+            key = lax.broadcasted_iota(jnp.int32, (n_keys, unit), 0)
+            qry = lax.broadcasted_iota(jnp.int32, (n_keys, unit), 1)
+            k_batch = key // (chips * unit) if kb is None else kb
+            k_tok = lax.rem(key, chips * unit) // sub * (BATCHES * sub) + lax.rem(key, sub) + k_batch * sub
+            ahead = qry // sub * (BATCHES * sub) + lax.rem(qry, sub) + b * sub - k_tok
             masks = [jnp.concatenate([ahead >= -unit_of(k) * chip_rows] * heads, axis=1) for k in ks]
-            flash(b, ks, *row_block(l, y, kb), masks)
+            flash(b, ks, *(whole_row(l, y) if kb is None else row_block(l, y, kb)), masks)
 
         def attn_out(b, p):
             def one(i, carry):
@@ -385,25 +402,36 @@
             ag2(A)
             ag0b(B)
             sides(qkv_l, A)
-            ag3(A)
-            qkv(l, B, OWN)
-            ag1(B)
-            qkv(l, A, OPP)
-
-            @pl.when(l == 0)
-            def _():
-                for r in range(n_sp - 1):
-                    @pl.when(r < y)
+            ahead = lax.max(y - 1, 0)
+            a_soon = jnp.where(l > 0, ahead, 0)
+            b_soon = jnp.where(l > 1, ahead, 0)
+            b_early = jnp.where(l > 0, ahead, 0)
+
+            def early(e, carry):
+                @pl.when(e == 1)
+                def _():
+                    ag3(A)
+                    qkv(l, B, OWN)
+                    ag1(B)
+                    qkv(l, A, OPP)
+
+                    @pl.when(l == 0)
                     def _():
-                        rdma(hot.at[r], hot.at[r], e_send.at[0], e_recv.at[r], sib).wait_recv()
-            kv_ready(l, A)
-
-            def early(p, carry):
-                attn_below(l, A, p, A)
-                attn_own(l, A, p, A)
+                        for r in range(n_sp - 1):
+                            @pl.when(r < y)
+                            def _():
+                                rdma(hot.at[r], hot.at[r], e_send.at[0], e_recv.at[r], sib).wait_recv()
+
+                a0, a1 = jnp.where(e == 0, 0, a_soon), jnp.where(e == 0, a_soon, y)
+                b0, b1 = jnp.where(e == 0, 0, b_soon), jnp.where(e == 0, b_soon, b_early)
+                kv_ready(l, A, a0, a1)
+                kv_ready(l, B, b0, b1)
+                attn_below(l, A, (RIGHT, LEFT, OWN), a0, a1, b0, b1)
                 return carry
 
             lax.fori_loop(0, 2, early, 0)
+            attn_below(l, A, (OPP,), 0, y, 0, b_early)
+            attn_own(l, A, (OPP, RIGHT, LEFT, OWN), A)
             ag2(B)
             sides(qkv_l, B)
             ag3(B)
@@ -414,12 +442,13 @@
                 cp.start()
 
             def late_a(p, carry):
-                attn_own(l, A, p, B)
+                ks = (2 * p, 2 * p + 1)
+                attn_own(l, A, ks, B)
 
                 @pl.when(p == 0)
                 def _():
-                    kv_ready(l, B)
-                attn_below(l, A, p, B)
+                    kv_ready(l, B, b_early, y)
+                attn_below(l, A, ks, 0, 0, b_early, y)
                 attn_out(A, p)
 
                 @pl.when(p == 0)
@@ -432,21 +461,21 @@
             ag_sent(B)
 
             def late_b(p, carry):
-                def keys(kb, carry):
-                    attn_below(l, B, p, kb)
-                    attn_own(l, B, p, kb)
-                    return carry
-
-                lax.fori_loop(0, BATCHES, keys, 0)
+                ks = (2 * p, 2 * p + 1)
+                attn_own(l, B, ks)
 
                 @pl.when(p == 0)
                 def _():
                     rs2b(A)
+                attn_below_rows(l, B, ks)
                 attn_out(B, p)
 
                 @pl.when(p == 0)
                 def _():
                     rs1(B)
+                    fin(A)
+                    norm(A, gain_row(gain_m, l))
+                    ag0a(A)
                 return carry
 
             lax.fori_loop(0, 2, late_b, 0)
@@ -455,10 +484,7 @@
             def _():
                 for cp in attn_weights(nxt):
                     cp.start()
-            fin(A)
-            norm(A, gain_row(gain_m, l))
             rs2a(B)
-            ag0a(A)
             for cp in mlp_weights(l)[:2]:
                 cp.wait()
             gate_up(A, OWN)
@@ -481,10 +507,17 @@
             rs1(A)
             down(A, 1)
             ag2(B)
-            gate_up(B, RIGHT)
-            rs2a(A)
-            ag3(B)
-            gate_up(B, OPP)
+
+            def two(i, carry):
+                gate_up(B, RIGHT - i)
+
+                @pl.when(i == 0)
+                def _():
+                    rs2a(A)
+                    ag3(B)
+                return carry
+
+            lax.fori_loop(0, 2, two, 0)
             ag_sent(B)
             down(B, 0)
             rs2b(A)
@@ -589,7 +622,7 @@
                 dma((n_tp,)), dma((n_tp,)), dma((n_tp,)), dma((n_tp,)), dma((n_sp - 1,)), dma((n_sp,)),
             ],
             compiler_params=pltpu.CompilerParams(collective_id=0, has_side_effects=True, vmem_limit_bytes=67_000_000),
-        )(hidden_in.reshape(BATCHES, sub, model_dim), tab, hot, attn_gain.astype(F32), mlp_gain.astype(F32),
+        )(hidden_in.reshape(BATCHES, sub, model_dim), tab, hot, attn_gain, mlp_gain,
           w_q, w_k, w_v, w_o, w_gate, w_up, w_down)
         cache_shape = (n_layers, n_rows, 1, HEAD_DIM)
         return out.reshape(tok_local, model_dim), k_c.reshape(cache_shape), v_c.reshape(cache_shape)

time: 548 us -> 521 us (0.951)
  Pallas kernels: 535 us -> 511 us
    pallas_call x1, Pallas kernels: 535 us -> 511 us  [device_fn(): pl.pallas_call(make_kernel(n_layers, n_sp, n_tp, sub, model_dim, q_dim, f...]
where the time goes in v3:
time: 521 us
  Pallas kernels  511 us (98%)
  local copies, waits for them, and re-layouts  7.41 us (1%)
    pallas_call x1, Pallas kernels, device_fn(): pl.pallas_call(make_kernel(n_layers, n_sp, n_tp, sub, model_dim, q_dim, f...  511 us

profile of v3, /device:TPU:120, one launch (start us, length us, event | category | flops | bytes accessed | tf_op | source)
XLA Modules:
  0.0 521.0 jit_solution(1092227659013471731)
XLA Ops:
  0.6 0.7 convert_element_type.14
  1.3 0.1 convert_element_type.15
  1.4 0.7 eq.15
  2.1 0.7 fusion.hot_own
  2.8 0.3 multiply_cosine_fusion
  3.1 0.7 pad_maximum_fusion.tab_own
  3.9 510.6 %decoder_stack.1 = (bf16[2,64,3072]{2,1,0:T(8,128)(2,1)}, bf16[4,4,2,2,64,128]{5,4,3,2,1,0:T(8,128)(2,1)}, bf16[4,4,2,2,64,128]{5,4,3,2,1,0:T(8,128)(2,1)}) custom-call(bf16[2,64,3072]{2,1,0:T(8,128)(2,1)} %bitcast.10, f32[2,64,128]{2,1,0:T(8,128)} %pad_maximum_fusion.tab_own, bf16[2,64,128]{2,1,0:T(8,128)(2,1)} %fusion.hot_own, bf16[4,3072]{1,0:T(4,128)(2,1)} %gain_a.1, ...), custom_call_target="tpu_custom_call" | custom-call | tf_op jit(solution)/shard_map/decoder_stack/pallas_call | solution.py:592
  514.4 2.1 copy.20
  516.5 2.3 copy.21
  518.7 2.3 copy.22
  (1 shorter events, 0.0 us)

commit v4 on v3

--- a/solution.py
+++ b/solution.py
@@ -558,6 +558,20 @@
                 hot_copy(d).wait_send()
 
     return kernel
+
+
+def place(*refs):
+    n = (len(refs) - 2) // 3
+    src, dst, buf, sem_in, sem_out = refs[:n], refs[n:2 * n], refs[2 * n:3 * n], refs[-2], refs[-1]
+    ins = [pltpu.make_async_copy(src[i], buf[i], sem_in.at[i]) for i in range(n)]
+    outs = [pltpu.make_async_copy(buf[i], dst[i], sem_out.at[i]) for i in range(n)]
+    for cp in ins:
+        cp.start()
+    for i in range(n):
+        ins[i].wait()
+        outs[i].start()
+    for cp in outs:
+        cp.wait()
 
 
 def solution(mesh):
@@ -624,6 +638,15 @@
             compiler_params=pltpu.CompilerParams(collective_id=0, has_side_effects=True, vmem_limit_bytes=67_000_000),
         )(hidden_in.reshape(BATCHES, sub, model_dim), tab, hot, attn_gain, mlp_gain,
           w_q, w_k, w_v, w_o, w_gate, w_up, w_down)
+        results = [out, k_c, v_c]
+        out, k_c, v_c = pl.pallas_call(
+            place,
+            name='place_results',
+            out_shape=[jax.ShapeDtypeStruct(r.shape, r.dtype) for r in results],
+            in_specs=[hbm] * 3,
+            out_specs=[hbm] * 3,
+            scratch_shapes=[pltpu.VMEM(r.shape, r.dtype) for r in results] + [dma((3,)), dma((3,))],
+        )(*results)
         cache_shape = (n_layers, n_rows, 1, HEAD_DIM)
         return out.reshape(tok_local, model_dim), k_c.reshape(cache_shape), v_c.reshape(cache_shape)
 

time: 521 us -> 517 us (level)
  local copies, waits for them, and re-layouts: 7.41 us -> 0.82 us
    unnamed x3 -> x0, local copies, waits for them, and re-layouts: 6.59 us -> none
where the time goes in v4:
time: 517 us
  Pallas kernels  513 us (99%)
    pallas_call x1, Pallas kernels, device_fn(): pl.pallas_call(make_kernel(n_layers, n_sp, n_tp, sub, model_dim, q_dim, f...  511 us

profile of v4, /device:TPU:120, one launch (start us, length us, event | category | flops | bytes accessed | tf_op | source)
XLA Modules:
  0.0 517.2 jit_solution(14726637308296279265)
XLA Ops:
  0.6 0.7 convert_element_type.14
  1.3 0.1 convert_element_type.15
  1.4 0.7 eq.15
  2.1 0.7 fusion.hot_own
  2.8 0.3 multiply_cosine_fusion
  3.1 0.7 pad_maximum_fusion.tab_own
  3.9 510.6 %decoder_stack.1 = (bf16[2,64,3072]{2,1,0:T(8,128)(2,1)}, bf16[4,4,2,2,64,128]{5,4,3,2,1,0:T(8,128)(2,1)}, bf16[4,4,2,2,64,128]{5,4,3,2,1,0:T(8,128)(2,1)}) custom-call(bf16[2,64,3072]{2,1,0:T(8,128)(2,1)} %bitcast.8, f32[2,64,128]{2,1,0:T(8,128)} %pad_maximum_fusion.tab_own, bf16[2,64,128]{2,1,0:T(8,128)(2,1)} %fusion.hot_own, bf16[4,3072]{1,0:T(4,128)(2,1)} %gain_a.1, ...), custom_call_target="tpu_custom_call" | custom-call | tf_op jit(solution)/shard_map/decoder_stack/pallas_call | solution.py:606
  514.4 2.8 place_results.1
  (1 shorter events, 0.0 us)
